TPU v7x, 128 devices: a whole 4x4x4 slice. The times are simulated.
128 devices in a mesh: dp: 1, col: 16 (over z, y), row: 8 (over x, core).
Axes of the slice: x: 4, y: 4, z: 4, core: 2. Of those that a mesh axis runs over, the one named last changes fastest.
Arguments:
- x_in: bfloat16 [4096, 4096], P(('dp', 'row'), 'col')
- w_qkv: bfloat16 [4096, 12288], P('row', 'col')
- w_out: bfloat16 [4096, 4096], P('row', 'col')
- doc_ids: int32 [4096], P(('dp', 'row'))
- grad_y: bfloat16 [4096, 4096], P(('dp', 'row'), 'col')
Outputs:
- output 1: bfloat16 [4096, 4096], P(('dp', 'row'), 'col')
- output 2: bfloat16 [4096, 12288], P(('dp', 'row'), 'col')
- output 3: bfloat16 [4096, 4096], P(('dp', 'row'), 'col')
All inputs are finite; a program needn't handle non-finite values.
Results may differ from a plain program's by a relative error of at most 0.00407559.
Values are sent between devices in bfloat16 or wider.
A program may use at most 1 GiB of HBM per device.

v0:
```python
import jax
import jax.numpy as jnp
from jax import lax
from jax.sharding import PartitionSpec as P

HEAD_DIM = 128


def solution(mesh):
    tok_spec = P(('dp', 'row'), 'col')
    mat_spec = P('row', 'col')
    seg_spec = P(('dp', 'row'))
    contract_last = (((1,), (1,)), ((), ()))
    contract_first = (((0,), (0,)), ((), ()))

    def grad_step(x_blk, wqkv_blk, wout_blk, seg_blk, dy_blk):
        seq_loc, width_loc = x_blk.shape
        n_loc = width_loc // HEAD_DIM
        sm_scale = HEAD_DIM ** -0.5
        x_row = lax.all_gather(x_blk, 'col', axis=1, tiled=True)
        w_col = lax.all_gather(wqkv_blk, 'row', axis=0, tiled=True)
        qkv_loc = jnp.dot(x_row, w_col, preferred_element_type=jnp.float32).astype(jnp.bfloat16)
        qkv_loc = qkv_loc.reshape(seq_loc, n_loc, 3, HEAD_DIM)
        q_loc = qkv_loc[:, :, 0]
        kv_all = lax.all_gather(qkv_loc[:, :, 1:], 'row', axis=0, tiled=True)
        k_all = kv_all[:, :, 0]
        v_all = kv_all[:, :, 1]
        seg_all = lax.all_gather(seg_blk, 'row', axis=0, tiled=True)
        wout_col = lax.all_gather(wout_blk, 'row', axis=0, tiled=True)
        do_part = lax.dot_general(dy_blk, wout_col, contract_last, preferred_element_type=jnp.float32)
        d_attn = lax.psum_scatter(do_part, 'col', scatter_dimension=1, tiled=True)
        d_attn = d_attn.astype(jnp.bfloat16).reshape(seq_loc, n_loc, HEAD_DIM)
        same_doc = seg_blk[:, None] == seg_all[None, :]
        scores = jnp.einsum('qhd,khd->hqk', q_loc, k_all, preferred_element_type=jnp.float32) * sm_scale
        scores = jnp.where(same_doc[None], scores, -jnp.inf)
        p_attn = jax.nn.softmax(scores, axis=-1)
        p_bf = p_attn.astype(jnp.bfloat16)
        attn_out = jnp.einsum('hqk,khd->qhd', p_bf, v_all, preferred_element_type=jnp.float32)
        attn_out = attn_out.astype(jnp.bfloat16).reshape(seq_loc, width_loc)
        d_probs = jnp.einsum('qhd,khd->hqk', d_attn, v_all, preferred_element_type=jnp.float32)
        row_dot = jnp.sum(p_attn * d_probs, axis=-1, keepdims=True)
        d_scores = (p_attn * (d_probs - row_dot) * sm_scale).astype(jnp.bfloat16)
        dq_loc = jnp.einsum('hqk,khd->qhd', d_scores, k_all, preferred_element_type=jnp.float32)
        dk_part = jnp.einsum('hqk,qhd->khd', d_scores, q_loc, preferred_element_type=jnp.float32)
        dv_part = jnp.einsum('hqk,qhd->khd', p_bf, d_attn, preferred_element_type=jnp.float32)
        dkv_loc = lax.psum_scatter(jnp.stack([dk_part, dv_part], axis=2), 'row', scatter_dimension=0, tiled=True)
        d_qkv = jnp.concatenate([dq_loc[:, :, None], dkv_loc], axis=2)
        d_qkv = d_qkv.astype(jnp.bfloat16).reshape(seq_loc, 3 * width_loc)
        dx_part = lax.dot_general(d_qkv, w_col, contract_last, preferred_element_type=jnp.float32)
        grad_x = lax.psum_scatter(dx_part, 'col', scatter_dimension=1, tiled=True).astype(jnp.bfloat16)
        dw_part = lax.dot_general(x_row, d_qkv, contract_first, preferred_element_type=jnp.float32)
        grad_wqkv = lax.psum_scatter(dw_part, 'row', scatter_dimension=0, tiled=True).astype(jnp.bfloat16)
        attn_row = lax.all_gather(attn_out, 'col', axis=1, tiled=True)
        dwo_part = lax.dot_general(attn_row, dy_blk, contract_first, preferred_element_type=jnp.float32)
        grad_wout = lax.psum_scatter(dwo_part, 'row', scatter_dimension=0, tiled=True).astype(jnp.bfloat16)
        return grad_x, grad_wqkv, grad_wout

    return jax.shard_map(grad_step, mesh=mesh, in_specs=(tok_spec, mat_spec, mat_spec, seg_spec, tok_spec), out_specs=(tok_spec, tok_spec, tok_spec), check_vma=False)
```

profile of v0, /device:TPU:1, one launch (start us, length us, event | category | flops | bytes accessed | tf_op | source)
XLA Modules:
  0.0 580.1 jit_solution(3977539123022100151)
XLA Ops:
  7.2 0.7 all-gather.7.cloned.1.call-update
  7.9 0.0 all-gather.9.cloned.1.call-start
  8.0 0.7 all-gather.9.cloned.1.call-update
  8.7 0.7 all-gather.13.cloned.1.call-update
  9.4 0.0 all-gather.11.cloned.1.call-start
  9.4 58.8 %all-gather.7.cloned.1.call-done = bf16[512,4096]{1,0:T(8,128)(2,1)} async-done(((bf16[512,256]{1,0:T(8,128)(2,1)}), bf16[512,4096]{1,0:T(8,128)(2,1)}) %all-gather.7.cloned.1.call-update) | async-done | bytes 4194320 | tf_op jit(solution)/shard_map/all_gather | solution.py:20
  68.3 43.3 %all-gather.9.cloned.1.call-done = bf16[4096,768]{1,0:T(8,128)(2,1)} async-done(((bf16[512,768]{1,0:T(8,128)(2,1)}), bf16[4096,768]{1,0:T(8,128)(2,1)}) %all-gather.9.cloned.1.call-update) | async-done | bytes 6291472 | tf_op jit(solution)/shard_map/all_gather | solution.py:21
  111.5 7.5 %convolution_convert_fusion = bf16[512,768]{1,0:T(8,128)(2,1)S(1)} fusion(bf16[512,4096]{1,0:T(8,128)(2,1)} %all-gather.7.cloned.1.call-done, bf16[4096,768]{1,0:T(8,128)(2,1)} %all-gather.9.cloned.1.call-done), kind=kOutput, calls=%fused_computation.26 | convolution fusion | flops 3221618688 | bytes 11272192 | tf_op jit(solution)/shard_map/dot_general | solution.py:22
  119.0 0.3 copy.26
  119.3 1.0 copy.39
  120.4 0.0 reduce-scatter.6.cloned.1.call-start
  120.4 18.1 %all-gather.13.cloned.1.call-done = bf16[4096,256]{1,0:T(8,128)(2,1)} async-done(((bf16[512,256]{1,0:T(8,128)(2,1)}), bf16[4096,256]{1,0:T(8,128)(2,1)}) %all-gather.13.cloned.1.call-update) | async-done | bytes 2097168 | tf_op jit(solution)/shard_map/all_gather | solution.py:29
  138.5 6.1 %fusion.39 = f32[512,4096]{1,0:T(8,128)} fusion(bf16[512,256]{1,0:T(8,128)(2,1)S(1)} %copy-done, bf16[4096,256]{1,0:T(8,128)(2,1)} %all-gather.13.cloned.1.call-done), kind=kOutput, calls=%fused_computation.39 | convolution fusion | flops 1073741824 | bytes 10747904 | tf_op jit(solution)/shard_map/dot_general | solution.py:30
  144.6 0.0 all-gather.15.cloned.1.call-start
  144.7 13.1 %all-gather = s32[8,1,512]{2,1,0:T(1,128)S(1)} all-gather(s32[1,1,512]{2,1,0:T(1,128)S(1)} %bitcast.63), channel_id=1, replica_groups=mesh['dp'=1,'col'=16,'row'=8] {'row'}, dimensions={0}, use_global_device_ids=true | all-gather | bytes 18432 | tf_op jit(solution)/shard_map/all_gather | solution.py:28
  157.7 1.3 broadcast_compare_fusion
  159.1 14.1 %all-gather.11.cloned.1.call-done = bf16[4096,2,2,128]{3,0,1,2:T(8,128)(2,1)} async-done(((bf16[512,2,2,128]{3,0,1,2:T(8,128)(2,1)}), bf16[4096,2,2,128]{3,0,1,2:T(8,128)(2,1)}) %all-gather.11.cloned.1.call-update) | async-done | bytes 4194320 | tf_op jit(solution)/shard_map/all_gather | solution.py:25
  173.1 4.0 fusion.21
  177.1 11.9 %fusion.38 = (f32[2,512]{1,0:T(2,128)S(1)}, f32[2,512,4096]{2,1,0:T(8,128)}) fusion(f32[2,512,4096]{2,1,0:T(8,128)S(1)} %fusion.21, pred[512,4096]{1,0:T(8,128)(4,1)S(1)} %broadcast_compare_fusion), kind=kOutput, calls=%fused_computation.38 | output fusion | flops 25169920 | bytes 35655680 | tf_op jit(solution)/shard_map/sub | solution.py:36
  189.0 9.4 %fusion.26 = bf16[2,128,512]{2,1,0:T(8,128)(2,1)} fusion(bf16[4096,2,2,128]{3,0,1,2:T(8,128)(2,1)S(1)} %copy-done.1, f32[2,512,4096]{2,1,0:T(8,128)} %get-tuple-element.13, f32[2,512]{1,0:T(2,128)S(1)} %get-tuple-element.12), kind=kOutput, calls=%fused_computation.28 | convolution fusion | flops 1082261504 | bytes 19140608 | tf_op jit(solution)/shard_map/hqk,khd->qhd/dot_general | solution.py:38
  198.5 0.3 reduce-scatter.8.cloned.1.call-start
  198.7 61.2 %reduce-scatter.6.cloned.1.call-done = f32[512,256]{1,0:T(8,128)} async-done(((f32[512,4096]{1,0:T(8,128)}), f32[512,256]{1,0:T(8,128)}) %reduce-scatter.6.cloned.1.call-update) | async-done | bytes 524304 | tf_op jit(solution)/shard_map/reduce_scatter | solution.py:31
  260.0 1.1 convert_element_type.33
  261.0 0.1 copy.41
  261.2 9.7 %fusion.22 = f32[2,512,4096]{2,1,0:T(8,128)} fusion(bf16[512,2,128]{0,2,1:T(8,128)(2,1)S(1)} %bitcast.57, bf16[4096,2,2,128]{3,0,1,2:T(8,128)(2,1)} %all-gather.11.cloned.1.call-done), kind=kOutput, calls=%fused_computation.25 | convolution fusion | flops 1073741824 | bytes 19136512 | tf_op jit(solution)/shard_map/qhd,khd->hqk/dot_general | solution.py:40
  270.9 27.5 %fusion.15 = f32[4096,2,1,128]{0,3,1,2:T(8,128)} fusion(f32[2,512,4096]{2,1,0:T(8,128)} %fusion.22, bf16[512,2,3,128]{0,3,2,1:T(8,128)(2,1)S(1)} %bitcast.56, f32[2,512,4096]{2,1,0:T(8,128)} %get-tuple-element.13, f32[2,512]{1,0:T(2,128)S(1)} %get-tuple-element.12), kind=kOutput, calls=%fused_computation.16 | convolution fusion | flops 1103107072 | bytes 71573504 | tf_op jit(solution)/shard_map/hqk,qhd->khd/dot_general | solution.py:44
  298.4 6.7 %convolution_bitcast_fusion.1 = f32[4096,2,1,128]{0,3,1,2:T(8,128)S(1)} fusion(bf16[512,2,128]{0,2,1:T(8,128)(2,1)S(1)} %bitcast.58, f32[2,512,4096]{2,1,0:T(8,128)} %get-tuple-element.13, f32[2,512]{1,0:T(2,128)S(1)} %get-tuple-element.12), kind=kOutput, calls=%fused_computation.17 | convolution fusion | flops 1082130432 | bytes 21237760 | tf_op jit(solution)/shard_map/hqk,qhd->khd/dot_general | solution.py:45
  305.1 0.2 copy-done.2
  305.3 3.7 pad_maximum_fusion
  309.1 0.0 reduce-scatter.14.cloned.1.call-start
  309.1 5.3 all-gather.15.cloned.1.call-done
  314.4 5.4 fusion.41
  319.9 0.0 reduce-scatter.10.cloned.1.call-start
  320.0 23.7 %fusion.29 = bf16[512,2,1,128]{0,3,1,2:T(8,128)(2,1)S(1)} fusion(f32[2,512,4096]{2,1,0:T(8,128)} %fusion.22, bf16[4096,2,2,128]{3,0,1,2:T(8,128)(2,1)} %all-gather.11.cloned.1.call-done, f32[2,512,4096]{2,1,0:T(8,128)} %get-tuple-element.13, f32[2,512]{1,0:T(2,128)S(1)} %get-tuple-element.12), kind=kOutput, calls=%fused_computation.29 | convolution fusion | flops 1103238144 | bytes 69476352 | tf_op jit(solution)/shard_map/hqk,khd->qhd/dot_general | solution.py:43
  343.6 25.1 %reduce-scatter.8.cloned.1.call-done = f32[512,2,2,128]{0,3,1,2:T(8,128)} async-done(((f32[4096,2,2,128]{0,3,1,2:T(8,128)}), f32[512,2,2,128]{0,3,1,2:T(8,128)}) %reduce-scatter.8.cloned.1.call-update) | async-done | bytes 1048592 | tf_op jit(solution)/shard_map/reduce_scatter | solution.py:46
  368.7 1.3 convert.9
  370.0 0.1 pad_maximum_fusion.1
  370.1 0.1 copy.33
  370.2 8.5 %fusion.40 = f32[512,4096]{1,0:T(8,128)} fusion(bf16[512,768]{0,1:T(8,128)(2,1)S(1)} %bitcast.59, bf16[4096,768]{1,0:T(8,128)(2,1)} %all-gather.9.cloned.1.call-done), kind=kOutput, calls=%fused_computation.40 | convolution fusion | flops 3221225472 | bytes 15466496 | tf_op jit(solution)/shard_map/dot_general | solution.py:49
  378.7 0.0 reduce-scatter.12.cloned.1.call-start
  378.7 8.5 %convolution_bitcast_fusion = f32[4096,768]{0,1:T(8,128)} fusion(bf16[512,768]{0,1:T(8,128)(2,1)S(1)} %bitcast.60, bf16[512,4096]{1,0:T(8,128)(2,1)} %all-gather.7.cloned.1.call-done), kind=kOutput, calls=%fused_computation.13 | convolution fusion | flops 3221225472 | bytes 17563648 | tf_op jit(solution)/shard_map/dot_general | solution.py:51
  387.3 19.0 %reduce-scatter.14.cloned.1.call-done = f32[512,256]{1,0:T(8,128)} async-done(((f32[4096,256]{1,0:T(8,128)}), f32[512,256]{1,0:T(8,128)}) %reduce-scatter.14.cloned.1.call-update) | async-done | bytes 524304 | tf_op jit(solution)/shard_map/reduce_scatter | solution.py:55
  406.3 1.8 convert_element_type.41
  408.0 87.4 %reduce-scatter.10.cloned.1.call-done = f32[512,256]{1,0:T(8,128)} async-done(((f32[512,4096]{1,0:T(8,128)}), f32[512,256]{1,0:T(8,128)}) %reduce-scatter.10.cloned.1.call-update) | async-done | bytes 524304 | tf_op jit(solution)/shard_map/reduce_scatter | solution.py:50
  495.5 1.8 convert_element_type.37
  497.2 73.4 %reduce-scatter.12.cloned.1.call-done = f32[512,768]{0,1:T(8,128)} async-done(((f32[4096,768]{0,1:T(8,128)}), f32[512,768]{0,1:T(8,128)}) %reduce-scatter.12.cloned.1.call-update) | async-done | bytes 1572880 | tf_op jit(solution)/shard_map/reduce_scatter | solution.py:52
  570.6 1.5 convert_element_type.38
  572.1 1.2 copy.35
  (17 shorter events, 0.2 us)
Async XLA Ops:
  7.2 131.3 %copy-start = (bf16[512,256]{1,0:T(8,128)(2,1)S(1)}, bf16[512,256]{1,0:T(8,128)(2,1)}, u32[]{:S(2)}) copy-start(bf16[512,256]{1,0:T(8,128)(2,1)} %param.9) | copy-start | bytes 786436
  7.2 61.1 %all-gather.7.cloned.1.call-start = ((), (), s32[]{:S(2)}) async-start(), calls=%async_computation.5 | async-start | bytes 4456448 | tf_op jit(solution)/shard_map/all_gather | solution.py:20
  7.9 103.6 %all-gather.9.cloned.1.call-start = ((), (), s32[]{:S(2)}) async-start(), calls=%async_computation.6 | async-start | bytes 7077888 | tf_op jit(solution)/shard_map/all_gather | solution.py:21
  8.7 129.8 %all-gather.13.cloned.1.call-start = ((), (), s32[]{:S(2)}) async-start(), calls=%async_computation.8 | async-start | bytes 2359296 | tf_op jit(solution)/shard_map/all_gather | solution.py:29
  9.4 163.7 %all-gather.11.cloned.1.call-start = ((), (), s32[]{:S(2)}) async-start(), calls=%async_computation.7 | async-start | bytes 4718592 | tf_op jit(solution)/shard_map/all_gather | solution.py:25
  120.4 24.3 %copy-start.3 = (s32[512]{0:T(512)S(1)}, s32[512]{0:T(512)}, u32[]{:S(2)}) copy-start(s32[512]{0:T(512)} %param.8) | copy-start | bytes 6148
  120.4 139.6 %reduce-scatter.6.cloned.1.call-start = ((), (), s32[]{:S(2)}) async-start(), calls=%async_computation.9 | async-start | bytes 8912896 | tf_op jit(solution)/shard_map/reduce_scatter | solution.py:31
  144.6 169.8 %all-gather.15.cloned.1.call-start = ((), (), s32[]{:S(2)}) async-start(), calls=%async_computation.13 | async-start | bytes 4456448 | tf_op jit(solution)/shard_map/all_gather | solution.py:53
  177.1 11.9 %copy-start.1 = (bf16[4096,2,2,128]{3,0,1,2:T(8,128)(2,1)S(1)}, bf16[4096,2,2,128]{3,0,1,2:T(8,128)(2,1)}, u32[]{:S(2)}) copy-start(bf16[4096,2,2,128]{3,0,1,2:T(8,128)(2,1)} %all-gather.11.cloned.1.call-done) | copy-start | bytes 12582916
  198.5 170.3 %reduce-scatter.8.cloned.1.call-start = ((), (), s32[]{:S(2)}) async-start(), calls=%async_computation.10 | async-start | bytes 9437184 | tf_op jit(solution)/shard_map/reduce_scatter | solution.py:46
  298.4 7.0 %copy-start.2 = (f32[4096,2,1,128]{0,3,1,2:T(8,128)S(1)}, f32[4096,2,1,128]{0,3,1,2:T(8,128)}, u32[]{:S(2)}) copy-start(f32[4096,2,1,128]{0,3,1,2:T(8,128)} %fusion.15) | copy-start | bytes 12582916
  309.1 97.2 %reduce-scatter.14.cloned.1.call-start = ((), (), s32[]{:S(2)}) async-start(), calls=%async_computation.14 | async-start | bytes 4718592 | tf_op jit(solution)/shard_map/reduce_scatter | solution.py:55
  319.9 175.6 %reduce-scatter.10.cloned.1.call-start = ((), (), s32[]{:S(2)}) async-start(), calls=%async_computation.11 | async-start | bytes 8912896 | tf_op jit(solution)/shard_map/reduce_scatter | solution.py:50
  378.7 192.0 %reduce-scatter.12.cloned.1.call-start = ((), (), s32[]{:S(2)}) async-start(), calls=%async_computation.12 | async-start | bytes 14155776 | tf_op jit(solution)/shard_map/reduce_scatter | solution.py:52
Sparse Core Ops, SparseCore 0:
  10.1 58.1 all-gather.6
  69.9 41.5 all-gather.8
  113.3 25.1 all-gather.12
  140.6 32.4 all-gather.10
  176.4 83.5 reduce-scatter.5
  262.5 51.8 all-gather.14
  316.8 51.8 reduce-scatter.7
  371.1 35.1 reduce-scatter.13
  409.7 85.7 reduce-scatter.9
  497.7 72.8 reduce-scatter.11
where the time goes:
time: 581 us; the launch traced here: 580 us
  waiting for transfers between devices  408 us (70%)
  matrix products  117 us (20%)
  other arithmetic  24.4 us (4%)
  between operations  14.3 us (2%)
  blocking collectives  13.1 us (2%)
    reduce_scatter x1, waiting for transfers between devices, grad_step(): lax.psum_scatter(dx_part, 'col', scatter_dimension=1, tiled=True)  87.4 us
    reduce_scatter x1, waiting for transfers between devices, grad_step(): lax.psum_scatter(dw_part, 'row', scatter_dimension=0, tiled=True)  73.4 us
    reduce_scatter x1, waiting for transfers between devices, grad_step(): d_attn = lax.psum_scatter(do_part, 'col', scatter_dimension=1, tiled=True)  61.2 us
    all_gather x1, waiting for transfers between devices, grad_step(): x_row = lax.all_gather(x_blk, 'col', axis=1, tiled=True)  58.8 us
    all_gather x1, waiting for transfers between devices, grad_step(): w_col = lax.all_gather(wqkv_blk, 'row', axis=0, tiled=True)  43.3 us
    dot_general x1, matrix products, grad_step(): jnp.einsum('hqk,qhd->khd', d_scores, q_loc, preferred_element_type=jnp.fl...  27.5 us
    reduce_scatter x1, waiting for transfers between devices, grad_step(): lax.psum_scatter(jnp.stack([dk_part, dv_part], axis=2), 'row', scatter_di...  25.1 us
    dot_general x1, matrix products, grad_step(): jnp.einsum('hqk,khd->qhd', d_scores, k_all, preferred_element_type=jnp.fl...  23.7 us
  transfers between devices with their start and end apart: 10, of which 10 were waited for; matrix products, arithmetic and copies ran while one was open for 24% of the time, Pallas kernels for 0%

commit v1 on v0

v1 whole, which is shorter than its diff:
```python
import jax
import jax.numpy as jnp
from jax import lax
from jax.experimental import pallas as pl
from jax.experimental.pallas import tpu as pltpu
from jax.sharding import PartitionSpec as P

HEAD_DIM = 128
NR, NC = 8, 16
SB = 512
SCALE = HEAD_DIM ** -0.5
HB, LANE, QKV, HQKV = 256, 128, 768, 384
MESH = pl.DeviceIdType.MESH
BF = jnp.bfloat16
F32 = jnp.float32
NT = (((1,), (1,)), ((), ()))
TN = (((0,), (0,)), ((), ()))
VLIM = 60 * 1024 * 1024


def dot(a, b, dims=None):
    if dims is None:
        dims = (((1,), (0,)), ((), ()))
    return lax.dot_general(a, b, dims, preferred_element_type=F32)


class Net:
    def __init__(self, send, recv):
        self.send, self.recv, self.n = send, recv, 0
        self.c, self.r = lax.axis_index('col'), lax.axis_index('row')
        self.x, self.core = self.r // 2, self.r % 2
        self.z, self.y = self.c // 4, self.c % 4
        self.sent = []

    def dev(self, axis, step):
        x, z, y, core = self.x, self.z, self.y, self.core
        if axis == 'x':
            x = (x + step) % 4
        elif axis == 'z':
            z = (z + step) % 4
        elif axis == 'y':
            y = (y + step) % 4
        else:
            core = 1 - core
        return {'col': z * 4 + y, 'row': x * 2 + core}

    def copy(self, src, dst, dev):
        i = self.n
        self.n += 1
        cp = pltpu.make_async_remote_copy(
            src_ref=src, dst_ref=dst, send_sem=self.send.at[i], recv_sem=self.recv.at[i],
            device_id=dev, device_id_type=MESH)
        cp.start()
        self.sent.append(cp)
        return cp

    def enter(self, axes, swap):
        bar = pltpu.get_barrier_semaphore()
        peers = []
        for a in axes:
            peers += [self.dev(a, 1), self.dev(a, 3)] if a != 'core' else [self.dev(a, 1)]
        for d in peers:
            pl.semaphore_signal(bar, inc=1, device_id=d, device_id_type=MESH)
        if swap:
            for k in range(2):
                @pl.when(jnp.logical_not(self.own_swap(k)))
                def _():
                    pl.semaphore_signal(bar, inc=1, device_id=self.swap_dev(k), device_id_type=MESH)
            n = len(peers) + 2 - (self.c // 2 == self.r).astype(jnp.int32)
            pl.semaphore_wait(bar, n)
        else:
            pl.semaphore_wait(bar, len(peers))

    def own_swap(self, k):
        return jnp.logical_and(self.c // 2 == self.r, self.c % 2 == k)

    def swap_dev(self, k):
        return {'col': 2 * self.r + k, 'row': self.c // 2}

    def finish(self):
        for cp in self.sent:
            cp.wait_send()


def swap_steps(net, src, dst, base):
    i = net.c % 2

    def cp(k, slot):
        return pltpu.make_async_remote_copy(
            src_ref=src.at[k], dst_ref=dst.at[slot], send_sem=net.send.at[base + k],
            recv_sem=net.recv.at[base + slot], device_id=net.swap_dev(k), device_id_type=MESH)

    for k in range(2):
        own = net.own_swap(k)

        @pl.when(jnp.logical_not(own))
        def _():
            cp(k, i).start()

        @pl.when(own)
        def _():
            dst[k] = src[k]
    yield
    for k in range(2):
        @pl.when(jnp.logical_not(net.own_swap(k)))
        def _():
            cp(k, k).wait_recv()
    net.tail.append(lambda: [pl.when(jnp.logical_not(net.own_swap(k)))(lambda k=k: cp(k, k).wait_send()) for k in range(2)])


def row_steps(net, src, out, half, local):
    x, core = net.x, net.core
    slot = lambda s: out.at[((x + s) % 4) * 2 + core]
    me = out.at[net.r]
    right, left, mate = net.dev('x', 1), net.dev('x', 3), net.dev('core', 1)
    a = net.copy(src, me, right)
    b = net.copy(src, me, left)
    got = [net.copy(src, me, mate)]
    own = pltpu.make_async_copy(src, me, local)
    own.start()
    yield
    a.wait_recv()
    c = net.copy(half(slot(3), 0), half(slot(3), 0), right)
    got.append(net.copy(slot(3), slot(3), mate))
    b.wait_recv()
    d = net.copy(half(slot(1), 1), half(slot(1), 1), left)
    got.append(net.copy(slot(1), slot(1), mate))
    yield
    c.wait_recv()
    d.wait_recv()
    got.append(net.copy(slot(2), slot(2), mate))
    yield
    for g in got:
        g.wait_recv()
    own.wait()


def col_steps(net, src, out, h, local):
    first, second = ('y', 'z') if h == 0 else ('z', 'y')
    z, y = net.z, net.y

    def one(s):
        return out.at[z, (y + s) % 4, h] if h == 0 else out.at[(z + s) % 4, y, h]

    def four(s):
        return out.at[(z + s) % 4, pl.ds(0, 4), h] if h == 0 else out.at[pl.ds(0, 4), (y + s) % 4, h]

    def pair(s, k):
        return out.at[(z + s) % 4, pl.ds(2 * k, 2), h] if h == 0 else out.at[pl.ds(2 * k, 2), (y + s) % 4, h]

    def rows(ref, k):
        return ref.at[pl.ds(k * LANE, LANE)]

    right, left = net.dev(first, 1), net.dev(first, 3)
    a = net.copy(src.at[h], one(0), right)
    b = net.copy(src.at[h], one(0), left)
    own = pltpu.make_async_copy(src.at[h], one(0), local)
    own.start()
    yield
    a.wait_recv()
    c = net.copy(rows(one(3), 0), rows(one(3), 0), right)
    b.wait_recv()
    d = net.copy(rows(one(1), 1), rows(one(1), 1), left)
    yield
    own.wait()
    c.wait_recv()
    d.wait_recv()
    right, left = net.dev(second, 1), net.dev(second, 3)
    a = net.copy(four(0), four(0), right)
    b = net.copy(four(0), four(0), left)
    yield
    a.wait_recv()
    c = net.copy(pair(3, 0), pair(3, 0), right)
    b.wait_recv()
    d = net.copy(pair(1, 1), pair(1, 1), left)
    yield
    c.wait_recv()
    d.wait_recv()


def drive(net, *groups):
    live = list(groups)
    while live:
        nxt = []
        for g in live:
            try:
                next(g)
                nxt.append(g)
            except StopIteration:
                pass
        live = nxt
    net.finish()
    for f in net.tail:
        f()


def later(steps, n):
    next(steps)
    yield
    for _ in range(n):
        yield
    yield from steps


def half_rows(n):
    return lambda ref, h: ref.at[pl.ds(h * n, n)]


def half_lead(ref, h):
    return ref.at[h]


def gather_in(x, dy, w, wo, seg, xg, dyg, wg, wog, segg, xt, dyt, wot, send, recv, local):
    net = Net(send, recv)
    net.tail = []
    net.enter(('x', 'z', 'y', 'core'), True)
    net.n = 6

    def wo_all():
        yield from swap_steps(net, wo, wot, 0)
        yield from later(row_steps(net, wot, wog, half_lead, local.at[0]), 1)

    drive(net,
          wo_all(),
          col_steps(net, x, xg, 0, local.at[1]), col_steps(net, x, xg, 1, local.at[2]),
          col_steps(net, dy, dyg, 0, local.at[5]), col_steps(net, dy, dyg, 1, local.at[6]),
          later(row_steps(net, seg, segg, half_rows(4), local.at[4]), 1),
          later(row_steps(net, w, wg, half_rows(HB), local.at[3]), 1),
          later(swap_steps(net, x, xt, 2), 5), later(swap_steps(net, dy, dyt, 4), 5))


def gather_mid(qkvo, xt, dyt, ag, xtg, dytg, send, recv, local):
    net = Net(send, recv)
    net.tail = []
    net.enter(('x', 'z', 'y', 'core'), False)
    drive(net,
          col_steps(net, xt, xtg, 0, local.at[1]), col_steps(net, xt, xtg, 1, local.at[2]),
          col_steps(net, dyt, dytg, 0, local.at[3]), col_steps(net, dyt, dytg, 1, local.at[4]),
          later(row_steps(net, qkvo, ag, half_rows(HB), local.at[0]), 1))


def gather_out(o, st, og, sg, send, recv, local):
    net = Net(send, recv)
    net.tail = []
    net.enter(('x', 'core'), False)
    drive(net,
          row_steps(net, st, sg, lambda ref, h: ref.at[:, pl.ds(h * HB, HB)], local.at[0]),
          row_steps(net, o, og, half_rows(HB), local.at[1]))


def scatter_steps(net, h, dq, w, dx, s1, r1, s2, r2, own, r3, r4):
    first, second = ('z', 'y') if h == 0 else ('y', 'z')
    f, g = (net.z, net.y) if h == 0 else (net.y, net.z)

    def part(ft, gt):
        c = ft * 4 + gt if h == 0 else gt * 4 + ft
        wb = w[c // 2, pl.ds(pl.multiple_of((c % 2) * HB, HB), HB), :]
        return dot(dq[pl.ds(h * HB, HB), :], wb, NT)

    def fill(dst, ft, base):
        def body(j, _):
            dst[j] = part(ft, base + j)
            return 0
        lax.fori_loop(0, dst.shape[0], body, 0)

    right, left = net.dev(first, 1), net.dev(first, 3)
    fill(s1.at[0], (f + 2) % 4, 0)
    fill(s1.at[1], (f + 2) % 4, 2)
    a = net.copy(s1.at[0], r1.at[0], right)
    b = net.copy(s1.at[1], r1.at[1], left)
    yield
    fill(s2.at[0], (f + 1) % 4, 0)
    fill(s2.at[1], (f + 3) % 4, 0)
    yield
    a.wait_recv()

    def add0(j, _):
        s2[0, j] = s2[0, j] + r1[0, j]
        return 0
    lax.fori_loop(0, 2, add0, 0)
    b.wait_recv()

    def add1(j, _):
        s2[1, 2 + j] = s2[1, 2 + j] + r1[1, j]
        return 0
    lax.fori_loop(0, 2, add1, 0)
    a = net.copy(s2.at[0], r2.at[0], right)
    b = net.copy(s2.at[1], r2.at[1], left)
    fill(own, f, 0)
    yield
    a.wait_recv()
    b.wait_recv()

    def add2(j, _):
        own[j] = own[j] + r2[0, j] + r2[1, j]
        return 0
    lax.fori_loop(0, 4, add2, 0)
    right, left = net.dev(second, 1), net.dev(second, 3)
    go, gr, gl = (g + 2) % 4, (g + 1) % 4, (g + 3) % 4
    a = net.copy(own.at[go, pl.ds(0, LANE)], r3.at[0], right)
    b = net.copy(own.at[go, pl.ds(LANE, LANE)], r3.at[1], left)
    yield
    a.wait_recv()
    own[gr, pl.ds(0, LANE), :] = own[gr, pl.ds(0, LANE), :] + r3[0]
    b.wait_recv()
    own[gl, pl.ds(LANE, LANE), :] = own[gl, pl.ds(LANE, LANE), :] + r3[1]
    a = net.copy(own.at[gr], r4.at[0], right)
    b = net.copy(own.at[gl], r4.at[1], left)
    yield
    a.wait_recv()
    b.wait_recv()
    dx[h] = (own[g] + r4[0] + r4[1]).astype(BF)


def scatter_out(dq, w, dwo, dx, dqg, dwt, *scr):
    bufs, (send, recv, local) = scr[:14], scr[14:]
    net = Net(send, recv)
    net.tail = []
    net.enter(('x', 'z', 'y', 'core'), True)
    net.n = 2
    drive(net,
          later(row_steps(net, dq, dqg, half_rows(HB), local.at[0]), 2),
          scatter_steps(net, 0, dq, w, dx, *bufs[:7]), scatter_steps(net, 1, dq, w, dx, *bufs[7:]),
          later(swap_steps(net, dwo, dwt, 0), 3))


def project(x, w, dy, wo, out, acc, acc2):
    i = pl.program_id(0)

    @pl.when(i == 0)
    def _():
        acc[...] = jnp.zeros_like(acc)
        acc2[...] = jnp.zeros_like(acc2)

    acc[...] += dot(x[0].reshape(SB, HB), w[0, pl.ds(0, HB), :]) + dot(x[1].reshape(SB, HB), w[0, pl.ds(HB, HB), :])
    acc2[...] += dot(dy[0].reshape(SB, HB), wo[0, 0], NT) + dot(dy[1].reshape(SB, HB), wo[0, 1], NT)

    @pl.when(i == NR - 1)
    def _():
        out[:, pl.ds(0, QKV)] = acc[...].astype(BF)
        out[:, pl.ds(QKV, HB)] = acc2[...].astype(BF)


def doc_of(pos, c1, c2):
    return (pos >= c1).astype(jnp.int32) + (pos >= c2).astype(jnp.int32)


def bounds(r, c1, c2):
    p0, p1 = r * SB, r * SB + SB - 1
    lo = jnp.where(p0 >= c2, c2, jnp.where(p0 >= c1, c1, 0))
    hi = jnp.where(p1 >= c2, NR * SB, jnp.where(p1 >= c1, c2, c1))
    return lo // SB, (hi + SB - 1) // SB


def tile(t):
    return slice(t * LANE, (t + 1) * LANE)


def attend(cuts, ag, o, dq, st, s_scr, d_scr, m_scr, l_scr, e_scr, o_scr, q_scr):
    r = lax.axis_index('row')
    c1, c2 = cuts[0], cuts[1]
    lo, hi = bounds(r, c1, c2)
    qdoc = doc_of(r * SB + lax.broadcasted_iota(jnp.int32, (SB, LANE), 0), c1, c2)
    st[...] = jnp.zeros_like(st)
    for h in range(2):
        b = h * HQKV
        m_scr[...] = jnp.full(m_scr.shape, -jnp.inf, F32)
        l_scr[...] = jnp.zeros_like(l_scr)
        e_scr[...] = jnp.zeros_like(e_scr)
        o_scr[...] = jnp.zeros_like(o_scr)
        q_scr[...] = jnp.zeros_like(q_scr)

        def sweep1(kb, _):
            s = dot(ag[r, :, b:b + LANE], ag[kb, :, b + LANE:b + HB], NT) * SCALE
            m = m_scr[...]
            for t in range(4):
                kdoc = doc_of(kb * SB + t * LANE + lax.broadcasted_iota(jnp.int32, (1, LANE), 1), c1, c2)
                v = jnp.where(qdoc == kdoc, s[:, tile(t)], -jnp.inf)
                s_scr[kb, :, tile(t)] = v
                m = jnp.maximum(m, v)
            m_scr[...] = m
            return 0
        lax.fori_loop(lo, hi, sweep1, 0)
        m_scr[...] = jnp.broadcast_to(jnp.max(m_scr[...], axis=1, keepdims=True), m_scr.shape)

        def sweep2(kb, _):
            d = dot(ag[r, :, QKV + h * LANE:896 + h * LANE], ag[kb, :, b + HB:b + HQKV], NT)
            l, e, m = l_scr[...], e_scr[...], m_scr[...]
            for t in range(4):
                p = jnp.exp(s_scr[kb, :, tile(t)] - m)
                s_scr[kb, :, tile(t)] = p
                d_scr[kb, :, tile(t)] = d[:, tile(t)]
                l = l + p
                e = e + p * d[:, tile(t)]
            l_scr[...] = l
            e_scr[...] = e
            return 0
        lax.fori_loop(lo, hi, sweep2, 0)
        tot = jnp.sum(l_scr[...], axis=1, keepdims=True)
        dot_row = jnp.sum(e_scr[...], axis=1, keepdims=True) / tot
        lse = jnp.broadcast_to(m_scr[:, 0:1] + jnp.log(tot), m_scr.shape)
        st[h:h + 1, :] = jnp.transpose(lse)[0:1, :]
        l_scr[...] = jnp.broadcast_to(1.0 / tot, l_scr.shape)
        e_scr[...] = jnp.broadcast_to(dot_row, e_scr.shape)
        st[2 + h:3 + h, :] = jnp.transpose(e_scr[...])[0:1, :]

        def sweep3(kb, _):
            ps, ds = [], []
            for t in range(4):
                p = s_scr[kb, :, tile(t)] * l_scr[...]
                ps.append(p.astype(BF))
                ds.append((p * (d_scr[kb, :, tile(t)] - e_scr[...]) * SCALE).astype(BF))
            o_scr[...] += dot(jnp.concatenate(ps, axis=1), ag[kb, :, b + HB:b + HQKV])
            q_scr[...] += dot(jnp.concatenate(ds, axis=1), ag[kb, :, b + LANE:b + HB])
            return 0
        lax.fori_loop(lo, hi, sweep3, 0)
        o[:, h * LANE:(h + 1) * LANE] = o_scr[...].astype(BF)
        dq[:, h * LANE:(h + 1) * LANE] = q_scr[...].astype(BF)


def attend_t(cuts, ag, sg, dq, out, k_scr, v_scr):
    r = lax.axis_index('row')
    c1, c2 = cuts[0], cuts[1]
    lo, hi = bounds(r, c1, c2)
    kdoc = doc_of(r * SB + lax.broadcasted_iota(jnp.int32, (SB, LANE), 0), c1, c2)
    for h in range(2):
        b = h * HQKV
        k_scr[...] = jnp.zeros_like(k_scr)
        v_scr[...] = jnp.zeros_like(v_scr)

        def sweep(qb, _):
            q, do = ag[qb, :, b:b + LANE], ag[qb, :, QKV + h * LANE:896 + h * LANE]
            s = dot(ag[r, :, b + LANE:b + HB], q, NT) * SCALE
            d = dot(ag[r, :, b + HB:b + HQKV], do, NT)
            ps, ds = [], []
            for t in range(4):
                qdoc = doc_of(qb * SB + t * LANE + lax.broadcasted_iota(jnp.int32, (1, LANE), 1), c1, c2)
                v = s[:, tile(t)] - sg[qb, h:h + 1, tile(t)]
                p = jnp.exp(jnp.where(kdoc == qdoc, v, -jnp.inf))
                ps.append(p.astype(BF))
                ds.append((p * (d[:, tile(t)] - sg[qb, 2 + h:3 + h, tile(t)]) * SCALE).astype(BF))
            v_scr[...] += dot(jnp.concatenate(ps, axis=1), do)
            k_scr[...] += dot(jnp.concatenate(ds, axis=1), q)
            return 0
        lax.fori_loop(lo, hi, sweep, 0)
        out[:, b:b + LANE] = dq[:, h * LANE:(h + 1) * LANE]
        out[:, b + LANE:b + HB] = k_scr[...].astype(BF)
        out[:, b + HB:b + HQKV] = v_scr[...].astype(BF)


def weight_grad(xt, dq, out, acc):
    i = pl.program_id(0)

    @pl.when(i == 0)
    def _():
        acc[...] = jnp.zeros_like(acc)

    for k in range(2):
        acc[pl.ds(k * HB, HB), :] += (dot(xt[0, k], dq[0, pl.ds(0, HB), :], TN)
                                        + dot(xt[1, k], dq[0, pl.ds(HB, HB), :], TN))

    @pl.when(i == NR - 1)
    def _():
        out[...] = acc[...].astype(BF)


def out_grad(og, dyt, out, acc):
    i = pl.program_id(0)

    @pl.when(i == 0)
    def _():
        acc[...] = jnp.zeros_like(acc)

    for k in range(2):
        acc[k] += (dot(og[0, pl.ds(0, HB), :], dyt[0, k], TN)
                   + dot(og[0, pl.ds(HB, HB), :], dyt[1, k], TN))

    @pl.when(i == NR - 1)
    def _():
        out[...] = acc[...].astype(BF)


def vm():
    return pl.BlockSpec(memory_space=pltpu.VMEM)


def hb():
    return pl.BlockSpec(memory_space=pl.ANY)


def sds(shape, dtype=BF):
    return jax.ShapeDtypeStruct(shape, dtype)


def net_call(fn, args, outs, cid, copies, n_local, scratch=(), out_specs=None):
    return pl.pallas_call(
        fn, out_shape=outs, in_specs=[vm()] * len(args),
        out_specs=out_specs or [hb()] * len(outs),
        scratch_shapes=[*scratch, pltpu.SemaphoreType.DMA((copies,)), pltpu.SemaphoreType.DMA((copies,)),
                        pltpu.SemaphoreType.DMA((n_local,))],
        compiler_params=pltpu.CompilerParams(collective_id=cid, has_side_effects=True, vmem_limit_bytes=VLIM),
    )(*args)


def core_call(fn, args, out, scratch):
    specs = [pl.BlockSpec(memory_space=pltpu.SMEM)] + [vm()] * (len(args) - 1)
    return pl.pallas_call(
        fn, out_shape=out, in_specs=specs, out_specs=jax.tree.map(lambda _: vm(), out),
        scratch_shapes=scratch, compiler_params=pltpu.CompilerParams(vmem_limit_bytes=VLIM))(*args)


def step_call(fn, args, blocks, out, scratch):
    def spec(b):
        return pl.BlockSpec(b, lambda i, n=len(b): (i,) + (0,) * (n - 1))
    return pl.pallas_call(
        fn, grid=(NR,), out_shape=out, in_specs=[spec(b) for b in blocks],
        out_specs=pl.BlockSpec(out.shape, lambda i, n=len(out.shape): (0,) * n),
        scratch_shapes=scratch, compiler_params=pltpu.CompilerParams(vmem_limit_bytes=VLIM))(*args)


def grad_step(x_blk, wqkv_blk, wout_blk, seg_blk, dy_blk):
    x3, dy3, wo3 = (a.reshape(2, HB, HB) for a in (x_blk, dy_blk, wout_blk))
    seg8 = jnp.concatenate([seg_blk, seg_blk]).reshape(8, LANE)
    plane = (4, 4, 2, HB, HB)
    piece = (2, HB, HB)
    xg, dyg, wg, wog, segg, xt, dyt, _ = net_call(
        gather_in, (x3, dy3, wqkv_blk, wo3, seg8),
        (sds(plane), sds(plane), sds((NR, SB, QKV)), sds((NR,) + piece), sds((NR, 8, LANE), jnp.int32),
         sds(piece), sds(piece), sds(piece)),
        cid=1, copies=64, n_local=7, out_specs=[hb()] * 5 + [vm()] * 3)
    cuts = jnp.stack([jnp.sum(segg[:, :4] < 1, dtype=jnp.int32), jnp.sum(segg[:, :4] < 2, dtype=jnp.int32)])
    pair = (2, 2, HB, HB)
    qkvo = step_call(
        project, (xg.reshape((NC,) + piece), wg, dyg.reshape((NC,) + piece), wog),
        (pair, (1, SB, QKV), pair, (1,) + piece), sds((SB, 1024)),
        [pltpu.VMEM((SB, QKV), F32), pltpu.VMEM((SB, HB), F32)])
    ag, xtg, dytg = net_call(
        gather_mid, (qkvo, xt, dyt), (sds((NR, SB, 1024)), sds(plane), sds(plane)), cid=2, copies=48, n_local=5)
    row128 = pltpu.VMEM((SB, LANE), F32)
    o, dq, st = core_call(
        attend, (cuts, ag), (sds((SB, HB)), sds((SB, HB)), sds((8, SB), F32)),
        [pltpu.VMEM((NR, SB, SB), F32), pltpu.VMEM((NR, SB, SB), F32)] + [row128] * 5)
    og, sg = net_call(gather_out, (o, st), (sds((NR, SB, HB)), sds((NR, 8, SB), F32)), cid=3, copies=16, n_local=2)
    dqkv = core_call(attend_t, (cuts, ag, sg, dq), sds((SB, QKV)), [row128] * 2)
    dwo = step_call(out_grad, (og, dytg.reshape((NC,) + piece)), ((1, SB, HB), pair), sds(piece),
                    [pltpu.VMEM(piece, F32)])
    b2 = pltpu.VMEM((2, 2, HB, HB), F32)
    b4 = pltpu.VMEM((2, 4, HB, HB), F32)
    bufs = [b2, b2, b4, b4, pltpu.VMEM((4, HB, HB), F32), pltpu.VMEM((2, LANE, HB), F32), pltpu.VMEM((2, HB, HB), F32)]
    dx, dqg, dwt = net_call(
        scatter_out, (dqkv, wg, dwo), (sds(piece), sds((NR, SB, QKV)), sds(piece)),
        cid=4, copies=32, n_local=1, scratch=bufs * 2, out_specs=[vm(), hb(), vm()])
    dw = step_call(weight_grad, (xtg.reshape((NC,) + piece), dqg), (pair, (1, SB, QKV)), sds((SB, QKV)),
                   [pltpu.VMEM((SB, QKV), F32)])
    return dx.reshape(SB, HB), dw, dwt.reshape(SB, HB)


def solution(mesh):
    tok_spec = P(('dp', 'row'), 'col')
    mat_spec = P('row', 'col')
    seg_spec = P(('dp', 'row'))
    return jax.shard_map(grad_step, mesh=mesh, in_specs=(tok_spec, mat_spec, mat_spec, seg_spec, tok_spec),
                         out_specs=(tok_spec, tok_spec, tok_spec), check_vma=False)
```

time: 581 us -> 297 us (0.51)
  waiting for transfers between devices: 408 us -> 0 us
  Pallas kernels: 0 us -> 286 us
  matrix products: 117 us -> 0 us
  other arithmetic: 24.4 us -> 4.72 us
  between operations: 14.3 us -> 0.68 us
  blocking collectives: 13.1 us -> 0 us
    pallas_call x0 -> x9, Pallas kernels: none -> 286 us  [the longest x4 229 us: net_call(): pl.pallas_call(fn, out_shape=outs, in_specs=[vm()] * len(args), out_specs...]
    reduce_scatter x5 -> x0, waiting for transfers between devices: 266 us -> none  [the longest x1 87.4 us: grad_step(): lax.psum_scatter(dx_part, 'col', scatter_dimension=1, tiled=True)]
    all_gather x5 -> x0, waiting for transfers between devices: 140 us -> none  [the longest x1 58.8 us: grad_step(): x_row = lax.all_gather(x_blk, 'col', axis=1, tiled=True)]
    dot_general x11 -> x0, matrix products: 117 us -> none  [the longest x1 27.5 us: grad_step(): jnp.einsum('hqk,qhd->khd', d_scores, q_loc, preferred_element_type=jnp.fl...]
    all_gather x1 -> x0, blocking collectives: 13.1 us -> none  [grad_step(): seg_all = lax.all_gather(seg_blk, 'row', axis=0, tiled=True)]
    sub x1 -> x0, other arithmetic: 11.9 us -> none  [grad_step(): p_attn = jax.nn.softmax(scores, axis=-1)]
    convert_element_type x4 -> x0, other arithmetic: 6.11 us -> none  [the longest x1 1.77 us: grad_step(): lax.psum_scatter(dx_part, 'col', scatter_dimension=1, tiled=True)]
  transfers between devices with their start and end apart: 10 -> 0, of which waited for: 10 -> 0; matrix products, arithmetic and copies ran while one was open for 24% -> 0% of each run, Pallas kernels for 0% -> 0%
where the time goes in v1:
time: 297 us; the launch traced here: 293 us
  Pallas kernels  286 us (96%)
  other arithmetic  4.72 us (2%)
    pallas_call x4, Pallas kernels, net_call(): pl.pallas_call(fn, out_shape=outs, in_specs=[vm()] * len(args), out_specs...  229 us
    pallas_call x2, Pallas kernels, core_call(): pl.pallas_call(fn, out_shape=out, in_specs=specs, out_specs=jax.tree.map(...  29.4 us
    pallas_call x3, Pallas kernels, step_call(): pl.pallas_call(fn, grid=(NR,), out_shape=out, in_specs=[spec(b) for b in...  28.2 us

profile of v1, /device:TPU:1, one launch (start us, length us, event | category | flops | bytes accessed | tf_op | source)
XLA Modules:
  0.0 293.3 jit_solution(8959808515920203035)
XLA Ops:
  0.6 1.4 pad_add_fusion.seg
  2.0 84.9 %shard_map.76 = (bf16[4,4,2,256,256]{4,3,2,1,0:T(8,128)(2,1)}, bf16[4,4,2,256,256]{4,3,2,1,0:T(8,128)(2,1)}, bf16[8,512,768]{2,1,0:T(8,128)(2,1)}, bf16[8,2,256,...) custom-call(bf16[2,256,256]{2,1,0:T(8,128)(2,1)} %bitcast.18, ...), custom_call_target="tpu_custom_call" | custom-call | tf_op jit(solution)/shard_map/pallas_call | solution.py:496
  86.9 1.4 convert_reduce_fusion.1
  88.3 2.0 pad_add_fusion.1.cuts
  90.3 11.4 %shard_map.77.qkvo = bf16[512,1024]{1,0:T(8,128)(2,1)} custom-call(bf16[16,2,256,256]{3,2,1,0:T(8,128)(2,1)} %bitcast.12, bf16[8,512,768]{2,1,0:T(8,128)(2,1)} %get-tuple-element.23.w, bf16[16,2,256,256]{3,2,1,0:T(8,128)(2,1)} %bitcast.13, bf16[8,2,256,256]{3,2,1,0:T(8,128)(2,1)} %get-tuple-element.25.wo), custom_call_target="tpu_custom_call" | custom-call | tf_op jit(solution)/shard_map/pallas_call | solution.py:515
  101.7 53.7 %shard_map.78 = (bf16[8,512,1024]{2,1,0:T(8,128)(2,1)}, bf16[4,4,2,256,256]{4,3,2,1,0:T(8,128)(2,1)}, bf16[4,4,2,256,256]{4,3,2,1,0:T(8,128)(2,1)}) custom-call(bf16[512,1024]{1,0:T(8,128)(2,1)} %shard_map.77.qkvo, bf16[2,256,256]{2,1,0:T(8,128)(2,1)} %get-tuple-element.26.xt, bf16[2,256,256]{2,1,0:T(8,128)(2,1)} %get-tuple-element.27.dyt), custom_call_target="tpu_custom_call" | custom-call | tf_op jit(solution)/shard_map/pallas_call | solution.py:496
  155.3 16.3 %shard_map.79 = (bf16[512,256]{1,0:T(8,128)(2,1)}, bf16[512,256]{1,0:T(8,128)(2,1)}, f32[8,512]{1,0:T(8,128)}) custom-call(s32[2]{0:T(128)} %pad_add_fusion.1.cuts, bf16[8,512,1024]{2,1,0:T(8,128)(2,1)} %get-tuple-element.28.ag), custom_call_target="tpu_custom_call" | custom-call | tf_op jit(solution)/shard_map/pallas_call | solution.py:507
  171.6 23.3 %shard_map.80 = (bf16[8,512,256]{2,1,0:T(8,128)(2,1)}, f32[8,8,512]{2,1,0:T(8,128)}) custom-call(bf16[512,256]{1,0:T(8,128)(2,1)} %get-tuple-element.29.o, f32[8,512]{1,0:T(8,128)} %get-tuple-element.30.st), custom_call_target="tpu_custom_call" | custom-call | tf_op jit(solution)/shard_map/pallas_call | solution.py:496
  194.9 7.2 %shard_map.82.dwo = bf16[2,256,256]{2,1,0:T(8,128)(2,1)} custom-call(bf16[8,512,256]{2,1,0:T(8,128)(2,1)} %get-tuple-element.33.og, bf16[16,2,256,256]{3,2,1,0:T(8,128)(2,1)} %bitcast.14), custom_call_target="tpu_custom_call" | custom-call | tf_op jit(solution)/shard_map/pallas_call | solution.py:515
  202.2 13.1 %shard_map.81.dq = bf16[512,768]{1,0:T(8,128)(2,1)} custom-call(s32[2]{0:T(128)} %pad_add_fusion.1.cuts, bf16[8,512,1024]{2,1,0:T(8,128)(2,1)} %get-tuple-element.28.ag, f32[8,8,512]{2,1,0:T(8,128)} %get-tuple-element.31.sg, bf16[512,256]{1,0:T(8,128)(2,1)} %get-tuple-element.32.dq), custom_call_target="tpu_custom_call" | custom-call | tf_op jit(solution)/shard_map/pallas_call | solution.py:507
  215.3 66.9 %shard_map.83 = (bf16[2,256,256]{2,1,0:T(8,128)(2,1)}, bf16[8,512,768]{2,1,0:T(8,128)(2,1)}, bf16[2,256,256]{2,1,0:T(8,128)(2,1)}) custom-call(bf16[512,768]{1,0:T(8,128)(2,1)} %shard_map.81.dq, bf16[8,512,768]{2,1,0:T(8,128)(2,1)} %get-tuple-element.23.w, bf16[2,256,256]{2,1,0:T(8,128)(2,1)} %shard_map.82.dwo), custom_call_target="tpu_custom_call" | custom-call | tf_op jit(solution)/shard_map/pallas_call | solution.py:496
  282.2 0.0 copy-start.1
  282.2 0.0 copy-start
  282.2 9.6 %shard_map.84 = bf16[512,768]{1,0:T(8,128)(2,1)} custom-call(bf16[16,2,256,256]{3,2,1,0:T(8,128)(2,1)} %bitcast.15, bf16[8,512,768]{2,1,0:T(8,128)(2,1)} %get-tuple-element.37.dq), custom_call_target="tpu_custom_call" | custom-call | tf_op jit(solution)/shard_map/pallas_call | solution.py:515
  291.9 0.0 copy-done.1
  291.9 0.7 copy.10
  292.6 0.0 copy-done
  292.6 0.7 copy.11
Async XLA Ops:
  282.2 9.7 %copy-start.1 = (bf16[2,256,256]{2,1,0:T(8,128)(2,1)S(1)}, bf16[2,256,256]{2,1,0:T(8,128)(2,1)}, u32[]{:S(2)}) copy-start(bf16[2,256,256]{2,1,0:T(8,128)(2,1)} %get-tuple-element.35) | copy-start | bytes 786436
  282.2 10.4 %copy-start = (bf16[2,256,256]{2,1,0:T(8,128)(2,1)S(1)}, bf16[2,256,256]{2,1,0:T(8,128)(2,1)}, u32[]{:S(2)}) copy-start(bf16[2,256,256]{2,1,0:T(8,128)(2,1)} %get-tuple-element.38) | copy-start | bytes 786436

commit v2 on v1

v2 whole, which is shorter than its diff:
```python
import jax
import jax.numpy as jnp
from jax import lax
from jax.experimental import pallas as pl
from jax.experimental.pallas import tpu as pltpu
from jax.sharding import PartitionSpec as P

HEAD_DIM = 128
NR, NC = 8, 16
SB = 512
SCALE = HEAD_DIM ** -0.5
HB, LANE, QKV, HQKV = 256, 128, 768, 384
TOK = 32
MESH = pl.DeviceIdType.MESH
BF = jnp.bfloat16
F32 = jnp.float32
NT = (((1,), (1,)), ((), ()))
TN = (((0,), (0,)), ((), ()))
VLIM = 60 * 1024 * 1024


def dot(a, b, dims=None):
    if dims is None:
        dims = (((1,), (0,)), ((), ()))
    return lax.dot_general(a, b, dims, preferred_element_type=F32)


class Net:
    def __init__(self, send, recv):
        self.send, self.recv, self.n = send, recv, 0
        self.c, self.r = lax.axis_index('col'), lax.axis_index('row')
        self.x, self.core = self.r // 2, self.r % 2
        self.z, self.y = self.c // 4, self.c % 4
        self.sent = []

    def dev(self, axis, step):
        x, z, y, core = self.x, self.z, self.y, self.core
        if axis == 'x':
            x = (x + step) % 4
        elif axis == 'z':
            z = (z + step) % 4
        elif axis == 'y':
            y = (y + step) % 4
        else:
            core = 1 - core
        return {'col': z * 4 + y, 'row': x * 2 + core}

    def mate(self, k):
        return {'col': self.c, 'row': (self.r + k) % NR}

    def copy(self, src, dst, dev):
        i = self.n
        self.n += 1
        cp = pltpu.make_async_remote_copy(
            src_ref=src, dst_ref=dst, send_sem=self.send.at[i], recv_sem=self.recv.at[i],
            device_id=dev, device_id_type=MESH)
        cp.start()
        self.sent.append(cp)
        return cp

    def enter(self, axes, swap):
        bar = pltpu.get_barrier_semaphore()
        peers = []
        for a in axes:
            if a == 'row':
                peers += [self.mate(k) for k in range(1, NR)]
            else:
                peers += [self.dev(a, 1), self.dev(a, 3)] if a != 'core' else [self.dev(a, 1)]
        for d in peers:
            pl.semaphore_signal(bar, inc=1, device_id=d, device_id_type=MESH)
        if swap:
            for k in range(2):
                @pl.when(jnp.logical_not(self.own_swap(k)))
                def _():
                    pl.semaphore_signal(bar, inc=1, device_id=self.swap_dev(k), device_id_type=MESH)
            n = len(peers) + 2 - (self.c // 2 == self.r).astype(jnp.int32)
            pl.semaphore_wait(bar, n)
        else:
            pl.semaphore_wait(bar, len(peers))

    def own_swap(self, k):
        return jnp.logical_and(self.c // 2 == self.r, self.c % 2 == k)

    def swap_dev(self, k):
        return {'col': 2 * self.r + k, 'row': self.c // 2}

    def finish(self):
        for cp in self.sent:
            cp.wait_send()


def swap_steps(net, src, dst, base):
    i = net.c % 2

    def cp(k, slot):
        return pltpu.make_async_remote_copy(
            src_ref=src.at[k], dst_ref=dst.at[slot], send_sem=net.send.at[base + k],
            recv_sem=net.recv.at[base + slot], device_id=net.swap_dev(k), device_id_type=MESH)

    for k in range(2):
        own = net.own_swap(k)

        @pl.when(jnp.logical_not(own))
        def _():
            cp(k, i).start()

        @pl.when(own)
        def _():
            dst[k] = src[k]
    yield
    for k in range(2):
        @pl.when(jnp.logical_not(net.own_swap(k)))
        def _():
            cp(k, k).wait_recv()
    net.tail.append(lambda: [pl.when(jnp.logical_not(net.own_swap(k)))(lambda k=k: cp(k, k).wait_send()) for k in range(2)])


def row_steps(net, src, out, half, local):
    x, core = net.x, net.core
    slot = lambda s: out.at[((x + s) % 4) * 2 + core]
    me = out.at[net.r]
    right, left, mate = net.dev('x', 1), net.dev('x', 3), net.dev('core', 1)
    a = net.copy(src, me, right)
    b = net.copy(src, me, left)
    got = [net.copy(src, me, mate)]
    if local is None:
        me[...] = src[...]
    else:
        own = pltpu.make_async_copy(src, me, local)
        own.start()
    yield
    a.wait_recv()
    c = net.copy(half(slot(3), 0), half(slot(3), 0), right)
    got.append(net.copy(slot(3), slot(3), mate))
    b.wait_recv()
    d = net.copy(half(slot(1), 1), half(slot(1), 1), left)
    got.append(net.copy(slot(1), slot(1), mate))
    yield
    c.wait_recv()
    d.wait_recv()
    got.append(net.copy(slot(2), slot(2), mate))
    yield
    for g in got:
        g.wait_recv()
    if local is not None:
        own.wait()


def col_steps(net, src, out, h, n, local=None):
    first, second = ('y', 'z') if h == 0 else ('z', 'y')
    z, y = net.z, net.y

    def one(s):
        return out.at[z, (y + s) % 4, h] if h == 0 else out.at[(z + s) % 4, y, h]

    def four(s):
        return out.at[(z + s) % 4, pl.ds(0, 4), h] if h == 0 else out.at[pl.ds(0, 4), (y + s) % 4, h]

    def pair(s, k):
        return out.at[(z + s) % 4, pl.ds(2 * k, 2), h] if h == 0 else out.at[pl.ds(2 * k, 2), (y + s) % 4, h]

    def rows(ref, k):
        return ref.at[pl.ds(k * n, n)]

    right, left = net.dev(first, 1), net.dev(first, 3)
    a = net.copy(src.at[h], one(0), right)
    b = net.copy(src.at[h], one(0), left)
    if local is None:
        one(0)[...] = src[h]
    else:
        own = pltpu.make_async_copy(src.at[h], one(0), local)
        own.start()
    yield
    a.wait_recv()
    c = net.copy(rows(one(3), 0), rows(one(3), 0), right)
    b.wait_recv()
    d = net.copy(rows(one(1), 1), rows(one(1), 1), left)
    yield
    if local is not None:
        own.wait()
    c.wait_recv()
    d.wait_recv()
    right, left = net.dev(second, 1), net.dev(second, 3)
    a = net.copy(four(0), four(0), right)
    b = net.copy(four(0), four(0), left)
    yield
    a.wait_recv()
    c = net.copy(pair(3, 0), pair(3, 0), right)
    b.wait_recv()
    d = net.copy(pair(1, 1), pair(1, 1), left)
    yield
    c.wait_recv()
    d.wait_recv()


def half_rows(n):
    return lambda ref, h: ref.at[pl.ds(h * n, n)]


def half_lead(ref, h):
    return ref.at[h]


def exchange(net, full, part):
    lead, off = net.c // NR, pl.multiple_of((net.c % NR) * TOK, TOK)

    def piece(r):
        return full.at[r // 2, pl.ds((r % 2) * 2, 2), lead, pl.ds(off, TOK)]

    mine = part.at[net.r // 4, net.r % 4]
    got = []
    for k in range(1, NR):
        got.append(net.copy(piece((net.r + k) % NR), mine, net.mate(k)))
    part[net.r // 4, net.r % 4] = piece(net.r)[...]
    yield
    for g in got:
        g.wait_recv()


def front(x, dy, w, wo, seg, segg, wout, ag, ado, xtg, dytg,
          xg, dyg, wg, wog, wot, xt, dyt, acc, qkv, do, send, recv, local):
    net = Net(send, recv)
    net.tail = []
    net.enter(('row', 'z', 'y'), True)
    net.n = 2

    def both(src, out, n, loc=(None, None)):
        g = [col_steps(net, src, out, h, n, loc[h]) for h in range(2)]
        for _ in range(5):
            for a in g:
                next(a, None)
            yield

    def go(*gens):
        for g in gens:
            next(g, None)

    gx, gdy = both(x, xg, LANE), both(dy, dyg, LANE)
    gw = row_steps(net, w, wg, half_rows(HB), None)
    gs = row_steps(net, seg, segg, half_rows(4), local.at[0])
    gsw = swap_steps(net, wo, wot, 0)
    gwo = row_steps(net, wot, wog, half_lead, None)
    ex, ey = exchange(net, xg, xt), exchange(net, dyg, dyt)
    gxt = both(xt, xtg, 2, (local.at[1], local.at[2]))
    gdyt = both(dyt, dytg, 2, (local.at[3], local.at[4]))
    gq = row_steps(net, qkv, ag, half_rows(HB), local.at[5])
    gdo = row_steps(net, do, ado, half_rows(HB), local.at[6])

    go(gx, gs, gw, gsw, gx, gx, gdy, gsw, gs, gw, gwo, gs, gx, gdy, gw, gs, gw, gx, gdy, ex)
    keep = pltpu.make_async_copy(wg, wout, local.at[7])
    keep.start()
    go(gwo)

    def qkv_step(c, a):
        xb = xg[c // 4, c % 4].reshape(SB, HB)
        wb = wg[c // 2, pl.ds(pl.multiple_of((c % 2) * HB, HB), HB), :]
        acc[...] += dot(xb, wb)
        return a
    acc[...] = jnp.zeros_like(acc)
    lax.fori_loop(0, NC, qkv_step, 0)
    qkv[...] = acc[...].astype(BF)
    go(gwo, ex, gq, gxt, gwo, gdy, gxt, gdy, ey)

    def do_step(c, a):
        yb = dyg[c // 4, c % 4].reshape(SB, HB)
        acc[:, pl.ds(0, HB)] += dot(yb, wog[c // 2, c % 2], NT)
        return a
    acc[...] = jnp.zeros_like(acc)
    lax.fori_loop(0, NC, do_step, 0)
    do[...] = acc[:, pl.ds(0, HB)].astype(BF)
    go(ey, gxt, gdo, gdyt, gq, gdyt, gdo, gxt, gq, gdo, gxt, gdyt, gq, gdo, gdyt, gdyt)
    keep.wait()
    for g in (gx, gdy, gw, gs, gsw, gwo, ex, ey, gxt, gdyt, gq, gdo):
        for _ in g:
            pass
    net.finish()
    for f in net.tail:
        f()


def share(st, sg, send, recv, local):
    net = Net(send, recv)
    net.tail = []
    net.enter(('row',), False)
    mine = sg.at[net.r]
    own = pltpu.make_async_copy(st, mine, local.at[0])
    own.start()
    got = [net.copy(st, mine, net.mate(k)) for k in range(1, NR)]
    own.wait()
    for g in got:
        g.wait_recv()
    net.finish()


def scatter_steps(net, h, dq, w, dx, s1, r1, s2, r2, own, r3, r4):
    first, second = ('z', 'y') if h == 0 else ('y', 'z')
    f, g = (net.z, net.y) if h == 0 else (net.y, net.z)

    def part(ft, gt):
        c = ft * 4 + gt if h == 0 else gt * 4 + ft
        wb = w[c // 2, pl.ds(pl.multiple_of((c % 2) * HB, HB), HB), :]
        return dot(dq[pl.ds(h * HB, HB), :], wb, NT)

    def fill(dst, ft, base):
        def body(j, _):
            dst[j] = part(ft, base + j)
            return 0
        lax.fori_loop(0, dst.shape[0], body, 0)

    right, left = net.dev(first, 1), net.dev(first, 3)
    fill(s1.at[0], (f + 2) % 4, 0)
    fill(s1.at[1], (f + 2) % 4, 2)
    a = net.copy(s1.at[0], r1.at[0], right)
    b = net.copy(s1.at[1], r1.at[1], left)
    yield
    fill(s2.at[0], (f + 1) % 4, 0)
    a2 = net.copy(s2.at[0, pl.ds(2, 2)], r2.at[0, pl.ds(2, 2)], right)
    fill(s2.at[1], (f + 3) % 4, 0)
    b2 = net.copy(s2.at[1, pl.ds(0, 2)], r2.at[1, pl.ds(0, 2)], left)
    yield
    a.wait_recv()

    def add0(j, _):
        s2[0, j] = s2[0, j] + r1[0, j]
        return 0
    lax.fori_loop(0, 2, add0, 0)
    b.wait_recv()

    def add1(j, _):
        s2[1, 2 + j] = s2[1, 2 + j] + r1[1, j]
        return 0
    lax.fori_loop(0, 2, add1, 0)
    a = net.copy(s2.at[0, pl.ds(0, 2)], r2.at[0, pl.ds(0, 2)], right)
    b = net.copy(s2.at[1, pl.ds(2, 2)], r2.at[1, pl.ds(2, 2)], left)
    fill(own, f, 0)
    yield
    for cp in (a2, b2, a, b):
        cp.wait_recv()

    def add2(j, _):
        own[j] = own[j] + r2[0, j] + r2[1, j]
        return 0
    lax.fori_loop(0, 4, add2, 0)
    right, left = net.dev(second, 1), net.dev(second, 3)
    go, gr, gl = (g + 2) % 4, (g + 1) % 4, (g + 3) % 4
    up, low = pl.ds(0, LANE), pl.ds(LANE, LANE)
    a = net.copy(own.at[go, up], r3.at[0], right)
    b = net.copy(own.at[go, low], r3.at[1], left)
    a2 = net.copy(own.at[gr, low], r4.at[0, low], right)
    b2 = net.copy(own.at[gl, up], r4.at[1, up], left)
    yield
    a.wait_recv()
    own[gr, up, :] = own[gr, up, :] + r3[0]
    b.wait_recv()
    own[gl, low, :] = own[gl, low, :] + r3[1]
    a = net.copy(own.at[gr, up], r4.at[0, up], right)
    b = net.copy(own.at[gl, low], r4.at[1, low], left)
    yield
    for cp in (a2, b2, a, b):
        cp.wait_recv()
    dx[h] = (own[g] + r4[0] + r4[1]).astype(BF)


def back(dq, o, wg, xtg, dytg, dx, dw, dwt, *scr):
    bufs, (w, xt, dyt, og, dqg, acc, acco, dwo, send, recv, local) = scr[:14], scr[14:]
    loads = [pltpu.make_async_copy(a, b, local.at[i]) for i, (a, b) in enumerate(((wg, w), (dytg, dyt), (xtg, xt)))]
    for cp in loads:
        cp.start()
    net = Net(send, recv)
    net.tail = []
    net.enter(('x', 'z', 'y', 'core'), True)
    net.n = 2

    def go(*gens):
        for g in gens:
            next(g, None)

    gog = row_steps(net, o, og, half_rows(HB), None)
    gdq = row_steps(net, dq, dqg, half_rows(HB), None)
    rs0 = scatter_steps(net, 0, dq, w, dx, *bufs[:7])
    rs1 = scatter_steps(net, 1, dq, w, dx, *bufs[7:])
    gsw = swap_steps(net, dwo, dwt, 0)
    go(gog, gdq)
    loads[0].wait()
    go(rs0, rs1, rs0, rs1, gog, rs0, rs1, gog, gog)
    loads[1].wait()

    def tokens(ref, r, k):
        return ref[:, :, r // 4, r % 4, k].reshape(SB, HB)

    def dwo_step(r, a):
        for k in range(2):
            acco[k] += dot(og[r], tokens(dyt, r, k), TN)
        return a
    acco[...] = jnp.zeros_like(acco)
    lax.fori_loop(0, NR, dwo_step, 0)
    dwo[...] = acco[...].astype(BF)
    go(gdq, gsw, gdq, gdq)
    loads[2].wait()

    def dw_step(r, a):
        for k in range(2):
            acc[pl.ds(k * HB, HB), :] += dot(tokens(xt, r, k), dqg[r], TN)
        return a
    acc[...] = jnp.zeros_like(acc)
    lax.fori_loop(0, NR, dw_step, 0)
    go(rs0, rs1, rs0, rs1)
    dw[...] = acc[...].astype(BF)
    go(rs0, rs1, gsw)
    for g in (gog, gdq, rs0, rs1, gsw):
        for _ in g:
            pass
    net.finish()
    for f in net.tail:
        f()


def doc_of(pos, c1, c2):
    return (pos >= c1).astype(jnp.int32) + (pos >= c2).astype(jnp.int32)


def bounds(r, c1, c2):
    p0, p1 = r * SB, r * SB + SB - 1
    lo = jnp.where(p0 >= c2, c2, jnp.where(p0 >= c1, c1, 0))
    hi = jnp.where(p1 >= c2, NR * SB, jnp.where(p1 >= c1, c2, c1))
    return lo // SB, (hi + SB - 1) // SB


def cuts_of(seg):
    return [jnp.sum((seg[...] < d).astype(F32)).astype(jnp.int32) // 2 for d in (1, 2)]


def tile(t):
    return slice(t * LANE, (t + 1) * LANE)


def attend(seg, ag, ado, o, dq, st, s_scr, d_scr, m_scr, l_scr, e_scr, o_scr, q_scr):
    r = lax.axis_index('row')
    c1, c2 = cuts_of(seg)
    lo, hi = bounds(r, c1, c2)
    qdoc = doc_of(r * SB + lax.broadcasted_iota(jnp.int32, (SB, LANE), 0), c1, c2)
    st[...] = jnp.zeros_like(st)
    for h in range(2):
        b = h * HQKV
        m_scr[...] = jnp.full(m_scr.shape, -jnp.inf, F32)
        l_scr[...] = jnp.zeros_like(l_scr)
        e_scr[...] = jnp.zeros_like(e_scr)
        o_scr[...] = jnp.zeros_like(o_scr)
        q_scr[...] = jnp.zeros_like(q_scr)

        def sweep1(kb, _):
            s = dot(ag[r, :, b:b + LANE], ag[kb, :, b + LANE:b + HB], NT) * SCALE
            m = m_scr[...]
            for t in range(4):
                kdoc = doc_of(kb * SB + t * LANE + lax.broadcasted_iota(jnp.int32, (1, LANE), 1), c1, c2)
                v = jnp.where(qdoc == kdoc, s[:, tile(t)], -jnp.inf)
                s_scr[kb, :, tile(t)] = v
                m = jnp.maximum(m, v)
            m_scr[...] = m
            return 0
        lax.fori_loop(lo, hi, sweep1, 0)
        m_scr[...] = jnp.broadcast_to(jnp.max(m_scr[...], axis=1, keepdims=True), m_scr.shape)

        def sweep2(kb, _):
            d = dot(ado[r, :, h * LANE:(h + 1) * LANE], ag[kb, :, b + HB:b + HQKV], NT)
            l, e, m = l_scr[...], e_scr[...], m_scr[...]
            for t in range(4):
                p = jnp.exp(s_scr[kb, :, tile(t)] - m)
                s_scr[kb, :, tile(t)] = p
                d_scr[kb, :, tile(t)] = d[:, tile(t)]
                l = l + p
                e = e + p * d[:, tile(t)]
            l_scr[...] = l
            e_scr[...] = e
            return 0
        lax.fori_loop(lo, hi, sweep2, 0)
        tot = jnp.sum(l_scr[...], axis=1, keepdims=True)
        dot_row = jnp.sum(e_scr[...], axis=1, keepdims=True) / tot
        lse = jnp.broadcast_to(m_scr[:, 0:1] + jnp.log(tot), m_scr.shape)
        st[h:h + 1, :] = jnp.transpose(lse)[0:1, :]
        l_scr[...] = jnp.broadcast_to(1.0 / tot, l_scr.shape)
        e_scr[...] = jnp.broadcast_to(dot_row, e_scr.shape)
        st[2 + h:3 + h, :] = jnp.transpose(e_scr[...])[0:1, :]

        def sweep3(kb, _):
            ps, ds = [], []
            for t in range(4):
                p = s_scr[kb, :, tile(t)] * l_scr[...]
                ps.append(p.astype(BF))
                ds.append((p * (d_scr[kb, :, tile(t)] - e_scr[...]) * SCALE).astype(BF))
            o_scr[...] += dot(jnp.concatenate(ps, axis=1), ag[kb, :, b + HB:b + HQKV])
            q_scr[...] += dot(jnp.concatenate(ds, axis=1), ag[kb, :, b + LANE:b + HB])
            return 0
        lax.fori_loop(lo, hi, sweep3, 0)
        o[:, h * LANE:(h + 1) * LANE] = o_scr[...].astype(BF)
        dq[:, h * LANE:(h + 1) * LANE] = q_scr[...].astype(BF)


def attend_t(seg, ag, ado, sg, dq, out, k_scr, v_scr):
    r = lax.axis_index('row')
    c1, c2 = cuts_of(seg)
    lo, hi = bounds(r, c1, c2)
    kdoc = doc_of(r * SB + lax.broadcasted_iota(jnp.int32, (SB, LANE), 0), c1, c2)
    for h in range(2):
        b = h * HQKV
        k_scr[...] = jnp.zeros_like(k_scr)
        v_scr[...] = jnp.zeros_like(v_scr)

        def sweep(qb, _):
            q, do = ag[qb, :, b:b + LANE], ado[qb, :, h * LANE:(h + 1) * LANE]
            s = dot(ag[r, :, b + LANE:b + HB], q, NT) * SCALE
            d = dot(ag[r, :, b + HB:b + HQKV], do, NT)
            ps, ds = [], []
            for t in range(4):
                qdoc = doc_of(qb * SB + t * LANE + lax.broadcasted_iota(jnp.int32, (1, LANE), 1), c1, c2)
                v = s[:, tile(t)] - sg[qb, h:h + 1, tile(t)]
                p = jnp.exp(jnp.where(kdoc == qdoc, v, -jnp.inf))
                ps.append(p.astype(BF))
                ds.append((p * (d[:, tile(t)] - sg[qb, 2 + h:3 + h, tile(t)]) * SCALE).astype(BF))
            v_scr[...] += dot(jnp.concatenate(ps, axis=1), do)
            k_scr[...] += dot(jnp.concatenate(ds, axis=1), q)
            return 0
        lax.fori_loop(lo, hi, sweep, 0)
        out[:, b:b + LANE] = dq[:, h * LANE:(h + 1) * LANE]
        out[:, b + LANE:b + HB] = k_scr[...].astype(BF)
        out[:, b + HB:b + HQKV] = v_scr[...].astype(BF)


def vm():
    return pl.BlockSpec(memory_space=pltpu.VMEM)


def hb():
    return pl.BlockSpec(memory_space=pl.ANY)


def sds(shape, dtype=BF):
    return jax.ShapeDtypeStruct(shape, dtype)


def net_call(fn, args, outs, cid, copies, n_local, scratch=(), out_specs=None, in_specs=None):
    return pl.pallas_call(
        fn, out_shape=outs, in_specs=in_specs or [vm()] * len(args),
        out_specs=out_specs or [hb()] * len(outs),
        scratch_shapes=[*scratch, pltpu.SemaphoreType.DMA((copies,)), pltpu.SemaphoreType.DMA((copies,)),
                        pltpu.SemaphoreType.DMA((n_local,))],
        compiler_params=pltpu.CompilerParams(collective_id=cid, has_side_effects=True, vmem_limit_bytes=VLIM),
    )(*args)


def core_call(fn, args, out, scratch):
    specs = [vm()] * len(args)
    return pl.pallas_call(
        fn, out_shape=out, in_specs=specs, out_specs=jax.tree.map(lambda _: vm(), out),
        scratch_shapes=scratch, compiler_params=pltpu.CompilerParams(vmem_limit_bytes=VLIM))(*args)


def grad_step(x_blk, wqkv_blk, wout_blk, seg_blk, dy_blk):
    x3, dy3, wo3 = (a.reshape(2, HB, HB) for a in (x_blk, dy_blk, wout_blk))
    seg8 = jnp.concatenate([seg_blk, seg_blk]).reshape(8, LANE)
    piece = (2, HB, HB)
    part = (2, 4, 2, TOK, HB)
    gathered = (NC, NR, 2, TOK, HB)
    plane = pltpu.VMEM((4, 4) + piece, BF)
    segg, wg, ag, ado, xtg, dytg = net_call(
        front, (x3, dy3, wqkv_blk, wo3, seg8),
        (sds((NR, 8, LANE), jnp.int32), sds((NR, SB, QKV)), sds((NR, SB, QKV)), sds((NR, SB, HB)),
         sds((4, 4) + part), sds((4, 4) + part)),
        cid=1, copies=120, n_local=8,
        scratch=[plane, plane, pltpu.VMEM((NR, SB, QKV), BF), pltpu.VMEM((NR,) + piece, BF), pltpu.VMEM(piece, BF),
                 pltpu.VMEM(part, BF), pltpu.VMEM(part, BF), pltpu.VMEM((SB, QKV), F32),
                 pltpu.VMEM((SB, QKV), BF), pltpu.VMEM((SB, HB), BF)])
    row128 = pltpu.VMEM((SB, LANE), F32)
    o, dq, st = core_call(
        attend, (segg, ag, ado), (sds((SB, HB)), sds((SB, HB)), sds((8, SB), F32)),
        [pltpu.VMEM((NR, SB, SB), F32), pltpu.VMEM((NR, SB, SB), F32)] + [row128] * 5)
    sg, = net_call(share, (st,), (sds((NR, 8, SB), F32),), cid=3, copies=7, n_local=1)
    dqkv = core_call(attend_t, (segg, ag, ado, sg, dq), sds((SB, QKV)), [row128] * 2)
    b2, b4 = pltpu.VMEM((2,) + piece, F32), pltpu.VMEM((2, 4, HB, HB), F32)
    bufs = [b2, b2, b4, b4, pltpu.VMEM((4, HB, HB), F32), pltpu.VMEM((2, LANE, HB), F32), pltpu.VMEM(piece, F32)]
    tokens = pltpu.VMEM((4, 4) + part, BF)
    dx, dw, dwt = net_call(
        back, (dqkv, o, wg, xtg, dytg), (sds(piece), sds((SB, QKV)), sds(piece)), cid=4, copies=42, n_local=3,
        scratch=bufs * 2 + [pltpu.VMEM((NR, SB, QKV), BF), tokens, tokens, pltpu.VMEM((NR, SB, HB), BF),
                            pltpu.VMEM((NR, SB, QKV), BF), pltpu.VMEM((SB, QKV), F32), pltpu.VMEM(piece, F32),
                            pltpu.VMEM(piece, BF)],
        in_specs=[vm()] * 2 + [hb()] * 3, out_specs=[vm()] * 3)
    return dx.reshape(SB, HB), dw, dwt.reshape(SB, HB)


def solution(mesh):
    tok_spec = P(('dp', 'row'), 'col')
    mat_spec = P('row', 'col')
    seg_spec = P(('dp', 'row'))
    return jax.shard_map(grad_step, mesh=mesh, in_specs=(tok_spec, mat_spec, mat_spec, seg_spec, tok_spec),
                         out_specs=(tok_spec, tok_spec, tok_spec), check_vma=False)
```

time: 297 us -> 256 us (0.86); the launches traced: 293 us -> 260 us
  Pallas kernels: 286 us -> 252 us
  local copies, waits for them, and re-layouts: 1.41 us -> 5.4 us
  other arithmetic: 4.72 us -> 1.36 us
    pallas_call x7 -> x3, Pallas kernels: 257 us -> 223 us  [net_call(): pl.pallas_call(fn, out_shape=outs, in_specs=in_specs or [vm()] * len(args...]
    unnamed x6 -> x3, local copies, waits for them, and re-layouts: 1.41 us -> 5.4 us
where the time goes in v2:
time: 256 us; the launch traced here: 260 us
  Pallas kernels  252 us (98%)
  local copies, waits for them, and re-layouts  5.4 us (2%)
    pallas_call x3, Pallas kernels, net_call(): pl.pallas_call(fn, out_shape=outs, in_specs=in_specs or [vm()] * len(args...  223 us
    pallas_call x2, Pallas kernels, core_call(): pl.pallas_call(fn, out_shape=out, in_specs=specs, out_specs=jax.tree.map(...  29.4 us
    unnamed x3, local copies, waits for them, and re-layouts  5.4 us

profile of v2, /device:TPU:1, one launch (start us, length us, event | category | flops | bytes accessed | tf_op | source)
XLA Modules:
  0.0 259.9 jit_solution(405864112541347218)
XLA Ops:
  0.6 1.4 pad_add_fusion.seg
  2.0 132.9 %shard_map.76 = (s32[8,8,128]{2,1,0:T(8,128)}, bf16[8,512,768]{2,1,0:T(8,128)(2,1)}, bf16[8,512,768]{2,1,0:T(8,128)(2,1)}, bf16[8,512,256]{2,1,0:T(8,128)(2,1)},...) custom-call(bf16[2,256,256]{2,1,0:T(8,128)(2,1)} %bitcast.8, ...), custom_call_target="tpu_custom_call" | custom-call | tf_op jit(solution)/shard_map/pallas_call | solution.py:542
  134.8 16.3 %shard_map.77 = (bf16[512,256]{1,0:T(8,128)(2,1)}, bf16[512,256]{1,0:T(8,128)(2,1)}, f32[8,512]{1,0:T(8,128)}) custom-call(s32[8,8,128]{2,1,0:T(8,128)} %get-tuple-element.15.seg, bf16[8,512,768]{2,1,0:T(8,128)(2,1)} %get-tuple-element.16.ag, bf16[8,512,256]{2,1,0:T(8,128)(2,1)} %get-tuple-element.17.ado), custom_call_target="tpu_custom_call" | custom-call | tf_op jit(solution)/shard_map/pallas_call | solution.py:553
  151.2 13.2 %shard_map.78.sg = f32[8,8,512]{2,1,0:T(8,128)} custom-call(f32[8,512]{1,0:T(8,128)} %get-tuple-element.18.st), custom_call_target="tpu_custom_call" | custom-call | tf_op jit(solution)/shard_map/pallas_call | solution.py:542
  164.3 13.1 %shard_map.79.dq = bf16[512,768]{1,0:T(8,128)(2,1)} custom-call(s32[8,8,128]{2,1,0:T(8,128)} %get-tuple-element.15.seg, bf16[8,512,768]{2,1,0:T(8,128)(2,1)} %get-tuple-element.16.ag, bf16[8,512,256]{2,1,0:T(8,128)(2,1)} %get-tuple-element.17.ado, f32[8,8,512]{2,1,0:T(8,128)} %shard_map.78.sg, bf16[512,256]{1,0:T(8,128)(2,1)} %get-tuple-element.19.dq), custom_call_target="tpu_custom_call" | custom-call | tf_op jit(solution)/shard_map/pallas_call | solution.py:553
  177.4 77.1 %shard_map.80 = (bf16[2,256,256]{2,1,0:T(8,128)(2,1)}, bf16[512,768]{1,0:T(8,128)(2,1)}, bf16[2,256,256]{2,1,0:T(8,128)(2,1)}) custom-call(bf16[512,768]{1,0:T(8,128)(2,1)} %shard_map.79.dq, bf16[512,256]{1,0:T(8,128)(2,1)} %get-tuple-element.20.o, bf16[8,512,768]{2,1,0:T(8,128)(2,1)} %get-tuple-element.21.wg, ...), custom_call_target="tpu_custom_call" | custom-call | tf_op jit(solution)/shard_map/pallas_call | solution.py:542
  254.5 1.7 copy.11
  256.2 2.1 copy.12
  258.2 1.7 copy.13

commit v3 on v2

--- a/solution.py
+++ b/solution.py
@@ -120,8 +120,10 @@
     slot = lambda s: out.at[((x + s) % 4) * 2 + core]
     me = out.at[net.r]
     right, left, mate = net.dev('x', 1), net.dev('x', 3), net.dev('core', 1)
-    a = net.copy(src, me, right)
-    b = net.copy(src, me, left)
+    a = [net.copy(half(src, 0), half(me, 0), right)]
+    b = [net.copy(half(src, 1), half(me, 1), left)]
+    a.append(net.copy(half(src, 1), half(me, 1), right))
+    b.append(net.copy(half(src, 0), half(me, 0), left))
     got = [net.copy(src, me, mate)]
     if local is None:
         me[...] = src[...]
@@ -129,13 +131,15 @@
         own = pltpu.make_async_copy(src, me, local)
         own.start()
     yield
-    a.wait_recv()
+    a[0].wait_recv()
     c = net.copy(half(slot(3), 0), half(slot(3), 0), right)
+    b[0].wait_recv()
+    d = net.copy(half(slot(1), 1), half(slot(1), 1), left)
+    yield
+    a[1].wait_recv()
     got.append(net.copy(slot(3), slot(3), mate))
-    b.wait_recv()
-    d = net.copy(half(slot(1), 1), half(slot(1), 1), left)
+    b[1].wait_recv()
     got.append(net.copy(slot(1), slot(1), mate))
-    yield
     c.wait_recv()
     d.wait_recv()
     got.append(net.copy(slot(2), slot(2), mate))
@@ -153,9 +157,6 @@
     def one(s):
         return out.at[z, (y + s) % 4, h] if h == 0 else out.at[(z + s) % 4, y, h]
 
-    def four(s):
-        return out.at[(z + s) % 4, pl.ds(0, 4), h] if h == 0 else out.at[pl.ds(0, 4), (y + s) % 4, h]
-
     def pair(s, k):
         return out.at[(z + s) % 4, pl.ds(2 * k, 2), h] if h == 0 else out.at[pl.ds(2 * k, 2), (y + s) % 4, h]
 
@@ -163,34 +164,38 @@
         return ref.at[pl.ds(k * n, n)]
 
     right, left = net.dev(first, 1), net.dev(first, 3)
-    a = net.copy(src.at[h], one(0), right)
-    b = net.copy(src.at[h], one(0), left)
+    a = [net.copy(rows(src.at[h], 0), rows(one(0), 0), right)]
+    b = [net.copy(rows(src.at[h], 1), rows(one(0), 1), left)]
+    a.append(net.copy(rows(src.at[h], 1), rows(one(0), 1), right))
+    b.append(net.copy(rows(src.at[h], 0), rows(one(0), 0), left))
     if local is None:
         one(0)[...] = src[h]
     else:
         own = pltpu.make_async_copy(src.at[h], one(0), local)
         own.start()
     yield
-    a.wait_recv()
+    a[0].wait_recv()
     c = net.copy(rows(one(3), 0), rows(one(3), 0), right)
-    b.wait_recv()
+    b[0].wait_recv()
     d = net.copy(rows(one(1), 1), rows(one(1), 1), left)
     yield
     if local is not None:
         own.wait()
-    c.wait_recv()
-    d.wait_recv()
+    for cp in (a[1], b[1], c, d):
+        cp.wait_recv()
     right, left = net.dev(second, 1), net.dev(second, 3)
-    a = net.copy(four(0), four(0), right)
-    b = net.copy(four(0), four(0), left)
-    yield
-    a.wait_recv()
+    a = [net.copy(pair(0, 0), pair(0, 0), right)]
+    b = [net.copy(pair(0, 1), pair(0, 1), left)]
+    a.append(net.copy(pair(0, 1), pair(0, 1), right))
+    b.append(net.copy(pair(0, 0), pair(0, 0), left))
+    yield
+    a[0].wait_recv()
     c = net.copy(pair(3, 0), pair(3, 0), right)
-    b.wait_recv()
+    b[0].wait_recv()
     d = net.copy(pair(1, 1), pair(1, 1), left)
     yield
-    c.wait_recv()
-    d.wait_recv()
+    for cp in (a[1], b[1], c, d):
+        cp.wait_recv()
 
 
 def half_rows(n):
@@ -246,7 +251,7 @@
     gq = row_steps(net, qkv, ag, half_rows(HB), local.at[5])
     gdo = row_steps(net, do, ado, half_rows(HB), local.at[6])
 
-    go(gx, gs, gw, gsw, gx, gx, gdy, gsw, gs, gw, gwo, gs, gx, gdy, gw, gs, gw, gx, gdy, ex)
+    go(gx, gs, gdy, gsw, gw, gx, gx, gdy, gsw, gs, gw, gwo, gx, gdy, gs, gx, ex, gw, gs, gw)
     keep = pltpu.make_async_copy(wg, wout, local.at[7])
     keep.start()
     go(gwo)
@@ -259,7 +264,7 @@
     acc[...] = jnp.zeros_like(acc)
     lax.fori_loop(0, NC, qkv_step, 0)
     qkv[...] = acc[...].astype(BF)
-    go(gwo, ex, gq, gxt, gwo, gdy, gxt, gdy, ey)
+    go(gq, gdy, ex, gxt, gwo, gwo, gdy, ey)
 
     def do_step(c, a):
         yb = dyg[c // 4, c % 4].reshape(SB, HB)
@@ -268,7 +273,7 @@
     acc[...] = jnp.zeros_like(acc)
     lax.fori_loop(0, NC, do_step, 0)
     do[...] = acc[:, pl.ds(0, HB)].astype(BF)
-    go(ey, gxt, gdo, gdyt, gq, gdyt, gdo, gxt, gq, gdo, gxt, gdyt, gq, gdo, gdyt, gdyt)
+    go(gdo, gxt, gxt, ey, gdyt, gq, gxt, gdyt, gdyt, gdo, gxt, gq, gdo, gdyt, gq, gdo, gdyt)
     keep.wait()
     for g in (gx, gdy, gw, gs, gsw, gwo, ex, ey, gxt, gdyt, gq, gdo):
         for _ in g:
@@ -403,8 +408,10 @@
             acc[pl.ds(k * HB, HB), :] += dot(tokens(xt, r, k), dqg[r], TN)
         return a
     acc[...] = jnp.zeros_like(acc)
-    lax.fori_loop(0, NR, dw_step, 0)
-    go(rs0, rs1, rs0, rs1)
+    go(rs0, rs1)
+    lax.fori_loop(0, NR // 2, dw_step, 0)
+    go(rs0, rs1)
+    lax.fori_loop(NR // 2, NR, dw_step, 0)
     dw[...] = acc[...].astype(BF)
     go(rs0, rs1, gsw)
     for g in (gog, gdq, rs0, rs1, gsw):
@@ -526,6 +533,11 @@
         out[:, b + HB:b + HQKV] = v_scr[...].astype(BF)
 
 
+def emit(*refs):
+    for i in range(3):
+        refs[3 + i][...] = refs[i][...]
+
+
 def vm():
     return pl.BlockSpec(memory_space=pltpu.VMEM)
 
@@ -566,7 +578,7 @@
         front, (x3, dy3, wqkv_blk, wo3, seg8),
         (sds((NR, 8, LANE), jnp.int32), sds((NR, SB, QKV)), sds((NR, SB, QKV)), sds((NR, SB, HB)),
          sds((4, 4) + part), sds((4, 4) + part)),
-        cid=1, copies=120, n_local=8,
+        cid=1, copies=162, n_local=8,
         scratch=[plane, plane, pltpu.VMEM((NR, SB, QKV), BF), pltpu.VMEM((NR,) + piece, BF), pltpu.VMEM(piece, BF),
                  pltpu.VMEM(part, BF), pltpu.VMEM(part, BF), pltpu.VMEM((SB, QKV), F32),
                  pltpu.VMEM((SB, QKV), BF), pltpu.VMEM((SB, HB), BF)])
@@ -580,12 +592,13 @@
     bufs = [b2, b2, b4, b4, pltpu.VMEM((4, HB, HB), F32), pltpu.VMEM((2, LANE, HB), F32), pltpu.VMEM(piece, F32)]
     tokens = pltpu.VMEM((4, 4) + part, BF)
     dx, dw, dwt = net_call(
-        back, (dqkv, o, wg, xtg, dytg), (sds(piece), sds((SB, QKV)), sds(piece)), cid=4, copies=42, n_local=3,
+        back, (dqkv, o, wg, xtg, dytg), (sds(piece), sds((SB, QKV)), sds(piece)), cid=4, copies=46, n_local=3,
         scratch=bufs * 2 + [pltpu.VMEM((NR, SB, QKV), BF), tokens, tokens, pltpu.VMEM((NR, SB, HB), BF),
                             pltpu.VMEM((NR, SB, QKV), BF), pltpu.VMEM((SB, QKV), F32), pltpu.VMEM(piece, F32),
                             pltpu.VMEM(piece, BF)],
         in_specs=[vm()] * 2 + [hb()] * 3, out_specs=[vm()] * 3)
-    return dx.reshape(SB, HB), dw, dwt.reshape(SB, HB)
+    small = sds((SB, HB))
+    return core_call(emit, (dx.reshape(SB, HB), dw, dwt.reshape(SB, HB)), (small, sds((SB, QKV)), small), [])
 
 
 def solution(mesh):

time: 256 us -> 240 us (0.938); the launches traced: 260 us -> 240 us
  Pallas kernels: 252 us -> 238 us
  local copies, waits for them, and re-layouts: 5.4 us -> 0 us
    pallas_call x3, Pallas kernels: 223 us -> 206 us  [net_call(): pl.pallas_call(fn, out_shape=outs, in_specs=in_specs or [vm()] * len(args...]
    unnamed x3 -> x0, local copies, waits for them, and re-layouts: 5.4 us -> none
    pallas_call x2 -> x3, Pallas kernels: 29.4 us -> 31.7 us  [core_call(): pl.pallas_call(fn, out_shape=out, in_specs=specs, out_specs=jax.tree.map(...]
where the time goes in v3:
time: 240 us
  Pallas kernels  238 us (99%)
    pallas_call x3, Pallas kernels, net_call(): pl.pallas_call(fn, out_shape=outs, in_specs=in_specs or [vm()] * len(args...  206 us
    pallas_call x3, Pallas kernels, core_call(): pl.pallas_call(fn, out_shape=out, in_specs=specs, out_specs=jax.tree.map(...  31.7 us

profile of v3, /device:TPU:1, one launch (start us, length us, event | category | flops | bytes accessed | tf_op | source)
XLA Modules:
  0.0 240.2 jit_solution(11661524345018390517)
XLA Ops:
  0.6 1.4 pad_add_fusion.seg
  2.0 119.2 %shard_map.76 = (s32[8,8,128]{2,1,0:T(8,128)}, bf16[8,512,768]{2,1,0:T(8,128)(2,1)}, bf16[8,512,768]{2,1,0:T(8,128)(2,1)}, bf16[8,512,256]{2,1,0:T(8,128)(2,1)},...) custom-call(bf16[2,256,256]{2,1,0:T(8,128)(2,1)} %bitcast.8, ...), custom_call_target="tpu_custom_call" | custom-call | tf_op jit(solution)/shard_map/pallas_call | solution.py:554
  121.2 16.3 %shard_map.77 = (bf16[512,256]{1,0:T(8,128)(2,1)}, bf16[512,256]{1,0:T(8,128)(2,1)}, f32[8,512]{1,0:T(8,128)}) custom-call(s32[8,8,128]{2,1,0:T(8,128)} %get-tuple-element.15.seg, bf16[8,512,768]{2,1,0:T(8,128)(2,1)} %get-tuple-element.16.ag, bf16[8,512,256]{2,1,0:T(8,128)(2,1)} %get-tuple-element.17.ado), custom_call_target="tpu_custom_call" | custom-call | tf_op jit(solution)/shard_map/pallas_call | solution.py:565
  137.6 16.3 %shard_map.78.sg = f32[8,8,512]{2,1,0:T(8,128)} custom-call(f32[8,512]{1,0:T(8,128)} %get-tuple-element.18.st), custom_call_target="tpu_custom_call" | custom-call | tf_op jit(solution)/shard_map/pallas_call | solution.py:554
  153.9 13.1 %shard_map.79.dq = bf16[512,768]{1,0:T(8,128)(2,1)} custom-call(s32[8,8,128]{2,1,0:T(8,128)} %get-tuple-element.15.seg, bf16[8,512,768]{2,1,0:T(8,128)(2,1)} %get-tuple-element.16.ag, bf16[8,512,256]{2,1,0:T(8,128)(2,1)} %get-tuple-element.17.ado, f32[8,8,512]{2,1,0:T(8,128)} %shard_map.78.sg, bf16[512,256]{1,0:T(8,128)(2,1)} %get-tuple-element.19.dq), custom_call_target="tpu_custom_call" | custom-call | tf_op jit(solution)/shard_map/pallas_call | solution.py:565
  167.0 70.9 %shard_map.80 = (bf16[2,256,256]{2,1,0:T(8,128)(2,1)}, bf16[512,768]{1,0:T(8,128)(2,1)}, bf16[2,256,256]{2,1,0:T(8,128)(2,1)}) custom-call(bf16[512,768]{1,0:T(8,128)(2,1)} %shard_map.79.dq, bf16[512,256]{1,0:T(8,128)(2,1)} %get-tuple-element.20.o, bf16[8,512,768]{2,1,0:T(8,128)(2,1)} %get-tuple-element.21.wg, ...), custom_call_target="tpu_custom_call" | custom-call | tf_op jit(solution)/shard_map/pallas_call | solution.py:554
  237.9 2.4 shard_map.81
